TPU v7x, 64 devices: a 2x2x8 block of a 4x4x8 slice. The times are simulated.
64 devices in a mesh: dp: 4 (over x, y), cp: 16 (over z, core).
Axes of the slice: x: 2, y: 2, z: 8, core: 2. Of those that a mesh axis runs over, the one named last changes fastest.
The devices are a block of a 4x4x8 slice.
Arguments:
- hidden: bfloat16 [32768, 2304], P(('dp', 'cp')), parts along dimension 0
- w_query: bfloat16 [6, 2304, 8, 256], replicated
- w_key: bfloat16 [6, 2304, 4, 256], replicated
- w_value: bfloat16 [6, 2304, 4, 256], replicated
- w_out: bfloat16 [6, 8, 256, 2304], replicated
Outputs:
- output: bfloat16 [32768, 2304], P(('dp', 'cp')), parts along dimension 0
There are 4 independent parts. A program takes and returns all parts, laid end to end along the dimension named above; an argument that names none is the same for every part.
All inputs are finite; a program needn't handle non-finite values.
Results may differ from a plain program's by a relative error of at most 0.0115828.
Values are sent between devices in bfloat16 or wider.
A program may use at most 768 MiB of HBM per device.

v0:
```python
import jax
import jax.numpy as jnp
from jax import lax
from jax.sharding import PartitionSpec as P

WINDOW = 1024
EPS_NORM = 1e-6
NEG_BIG = -1e30


def rms_normed(rows_in):
    widened = rows_in.astype(jnp.float32)
    return widened * lax.rsqrt(jnp.mean(widened * widened, axis=-1, keepdims=True) + EPS_NORM)


def project_qkv(hidden, w_query, w_key, w_value):
    normed = rms_normed(hidden).astype(jnp.bfloat16)
    queries = jnp.einsum("td,dhe->the", normed, w_query, preferred_element_type=jnp.float32).astype(jnp.bfloat16)
    key_rows = jnp.einsum("td,dhe->the", normed, w_key, preferred_element_type=jnp.float32).astype(jnp.bfloat16)
    value_rows = jnp.einsum("td,dhe->the", normed, w_value, preferred_element_type=jnp.float32).astype(jnp.bfloat16)
    return queries, key_rows, value_rows


def residual_update(hidden, attn_out, w_out):
    update = jnp.einsum("the,hed->td", attn_out, w_out, preferred_element_type=jnp.float32)
    return (hidden.astype(jnp.float32) + rms_normed(update)).astype(jnp.bfloat16)


def window_attention(queries, key_rows, value_rows, query_pos, key_pos):
    num_rows, num_heads, head_dim = queries.shape
    kv_heads = key_rows.shape[1]
    grouped = queries.reshape(num_rows, kv_heads, num_heads // kv_heads, head_dim)
    scores = jnp.einsum("qhgd,khd->hgqk", grouped, key_rows, preferred_element_type=jnp.float32) * head_dim ** -0.5
    offsets = key_pos[None, :] - query_pos[:, None]
    allowed = (offsets <= 0) & (offsets > -WINDOW) & (key_pos[None, :] >= 0)
    scores = jnp.where(allowed, scores, NEG_BIG)
    row_max = jnp.max(scores, axis=-1, keepdims=True)
    weights = jnp.exp(scores - row_max)
    row_sum = jnp.sum(weights, axis=-1)
    attn_out = jnp.einsum("hgqk,khd->hgqd", weights.astype(jnp.bfloat16), value_rows, preferred_element_type=jnp.float32)
    attn_out = attn_out / row_sum[..., None]
    return jnp.transpose(attn_out, (2, 0, 1, 3)).reshape(num_rows, num_heads, head_dim).astype(jnp.bfloat16)


def gather_halo(key_rows, value_rows, num_dev):
    tok_rows = key_rows.shape[0]
    piece_len = min(WINDOW, tok_rows)
    num_hops = WINDOW // piece_len
    tail_kv = jnp.stack([key_rows[tok_rows - piece_len:], value_rows[tok_rows - piece_len:]])
    pieces = []
    for hop_dist in range(num_hops, 0, -1):
        if hop_dist < num_dev:
            perm_pairs = [(source, source + hop_dist) for source in range(num_dev - hop_dist)]
            pieces.append(lax.ppermute(tail_kv, "cp", perm_pairs))
        else:
            pieces.append(jnp.zeros_like(tail_kv))
    halo_kv = jnp.concatenate(pieces, axis=1)
    return halo_kv[0], halo_kv[1]


def local_attention(queries, key_rows, value_rows, halo_keys, halo_values, dev_rank):
    tok_rows = queries.shape[0]
    block_len = tok_rows // 2
    all_keys = jnp.concatenate([halo_keys, key_rows], axis=0)
    all_values = jnp.concatenate([halo_values, value_rows], axis=0)
    key_span = WINDOW + block_len
    outputs = []
    for half_idx in range(2):
        start_row = half_idx * block_len
        query_pos = dev_rank * tok_rows + start_row + jnp.arange(block_len)
        key_pos = dev_rank * tok_rows - WINDOW + start_row + jnp.arange(key_span)
        outputs.append(window_attention(
            queries[start_row:start_row + block_len],
            all_keys[start_row:start_row + key_span],
            all_values[start_row:start_row + key_span],
            query_pos, key_pos))
    return jnp.concatenate(outputs, axis=0)


def output_owner(block_idx, num_dev):
    return block_idx if block_idx < num_dev else 2 * num_dev - 1 - block_idx


def to_output_layout(hidden, dev_rank, num_dev):
    block_len = hidden.shape[0] // 2
    even_pairs = [(source, output_owner(2 * source, num_dev)) for source in range(num_dev)]
    odd_pairs = [(source, output_owner(2 * source + 1, num_dev)) for source in range(num_dev)]
    from_even = lax.ppermute(hidden[:block_len], "cp", even_pairs)
    from_odd = lax.ppermute(hidden[block_len:], "cp", odd_pairs)
    is_even = dev_rank % 2 == 0
    lead_rows = jnp.where(is_even, from_even, from_odd)
    trail_rows = jnp.where(is_even, from_odd, from_even)
    return jnp.concatenate([lead_rows, trail_rows], axis=0)


def causal_block_attention(queries, block_id, kv_all, num_dev):
    block_len, num_heads, head_dim = queries.shape
    kv_heads = kv_all.shape[-2]
    group_size = num_heads // kv_heads
    grouped = queries.reshape(block_len, kv_heads, group_size, head_dim)
    query_pos = block_id * block_len + jnp.arange(block_len)
    zero_idx = jnp.zeros((), jnp.int32)

    def kv_step(key_block, state_in):
        row_max, row_sum, acc_out = state_in
        in_front = key_block < num_dev
        owner_dev = jnp.where(in_front, key_block, 2 * num_dev - 1 - key_block)
        half_idx = jnp.where(in_front, 0, 1).astype(jnp.int32)
        kv_block = lax.dynamic_slice(
            kv_all, (owner_dev, zero_idx, half_idx, zero_idx, zero_idx, zero_idx),
            (1, 2, 1, block_len, kv_heads, head_dim)).reshape(2, block_len, kv_heads, head_dim)
        scores = jnp.einsum("qhgd,khd->hgqk", grouped, kv_block[0], preferred_element_type=jnp.float32) * head_dim ** -0.5
        offsets = key_block * block_len + jnp.arange(block_len)[None, :] - query_pos[:, None]
        allowed = offsets <= 0
        scores = jnp.where(allowed, scores, NEG_BIG)
        new_max = jnp.maximum(row_max, jnp.max(scores, axis=-1))
        weights = jnp.where(allowed, jnp.exp(scores - new_max[..., None]), 0.0)
        rescale = jnp.exp(row_max - new_max)
        row_sum = row_sum * rescale + jnp.sum(weights, axis=-1)
        acc_out = acc_out * rescale[..., None] + jnp.einsum("hgqk,khd->hgqd", weights.astype(jnp.bfloat16), kv_block[1], preferred_element_type=jnp.float32)
        return new_max, row_sum, acc_out

    stat_shape = (kv_heads, group_size, block_len)
    init_state = (
        jnp.full(stat_shape, NEG_BIG, jnp.float32),
        jnp.zeros(stat_shape, jnp.float32),
        jnp.zeros(stat_shape + (head_dim,), jnp.float32),
    )
    row_max, row_sum, acc_out = lax.fori_loop(zero_idx, block_id + 1, kv_step, init_state)
    attn_out = acc_out / row_sum[..., None]
    return jnp.transpose(attn_out, (2, 0, 1, 3)).reshape(block_len, num_heads, head_dim).astype(jnp.bfloat16)


def global_layer(hidden, dev_rank, num_dev, weights):
    w_query, w_key, w_value, w_out = weights
    queries, key_rows, value_rows = project_qkv(hidden, w_query, w_key, w_value)
    tok_rows, kv_heads, head_dim = key_rows.shape
    block_len = tok_rows // 2
    kv_all = lax.all_gather(jnp.stack([key_rows, value_rows]), "cp")
    kv_all = kv_all.reshape(num_dev, 2, 2, block_len, kv_heads, head_dim)
    lead_out = causal_block_attention(queries[:block_len], dev_rank, kv_all, num_dev)
    trail_out = causal_block_attention(queries[block_len:], 2 * num_dev - 1 - dev_rank, kv_all, num_dev)
    return residual_update(hidden, jnp.concatenate([lead_out, trail_out], axis=0), w_out)


def solution(mesh):
    num_dev = mesh.shape["cp"]

    def per_device(hidden, w_query, w_key, w_value, w_out):
        dev_rank = lax.axis_index("cp")
        num_layers = w_query.shape[0]
        for layer_idx in range(num_layers - 1):
            queries, key_rows, value_rows = project_qkv(hidden, w_query[layer_idx], w_key[layer_idx], w_value[layer_idx])
            halo_keys, halo_values = gather_halo(key_rows, value_rows, num_dev)
            attn_out = local_attention(queries, key_rows, value_rows, halo_keys, halo_values, dev_rank)
            hidden = residual_update(hidden, attn_out, w_out[layer_idx])
        hidden = to_output_layout(hidden, dev_rank, num_dev)
        last_layer = num_layers - 1
        last_weights = (w_query[last_layer], w_key[last_layer], w_value[last_layer], w_out[last_layer])
        return global_layer(hidden, dev_rank, num_dev, last_weights)

    row_spec = P(("dp", "cp"), None)
    return jax.shard_map(per_device, mesh=mesh, in_specs=(row_spec, P(), P(), P(), P()), out_specs=row_spec, check_vma=False)
```

profile of v0, /device:TPU:21, one launch (start us, length us, event | category | flops | bytes accessed | tf_op | source)
XLA Modules:
  0.0 1177.1 jit_solution(728064650069629687)
XLA Ops:
  6.6 25.4 %fusion.436 = (bf16[1,2304,4,256]{3,2,1,0:T(4,128)(2,1)}, bf16[1,2304,4,256]{3,2,1,0:T(4,128)(2,1)}, bf16[1,2304,4,256]{3,2,1,0:T(4,128)(2,1)}, bf16[1,2304,4,25...) fusion(bf16[6,2304,4,256]{3,2,1,0:T(4,128)(2,1)} %param.11), kind=kLoop, calls=%fused_computation.503 | loop fusion | bytes 56623104 | tf_op jit(solution)/shard_map/slice | solution.py:159
  34.9 13.2 %fusion.437 = (bf16[1,2304,4,256]{3,2,1,0:T(4,128)(2,1)}, bf16[1,2304,4,256]{3,2,1,0:T(4,128)(2,1)}, bf16[1,2304,4,256]{3,2,1,0:T(4,128)(2,1)}, bf16[1,2304,4,25...) fusion(bf16[6,2304,4,256]{3,2,1,0:T(4,128)(2,1)S(1)} %copy-done.1), kind=kLoop, calls=%fused_computation.504 | loop fusion | bytes 56623104 | tf_op jit(solution)/shard_map/slice | solution.py:153
  48.1 5.8 fusion.346
  59.1 5.9 collective-permute-start
  68.3 38.4 %fusion.435 = (bf16[1,2304,8,256]{3,2,1,0:T(8,128)(2,1)}, bf16[1,2304,8,256]{3,2,1,0:T(8,128)(2,1)}, bf16[1,2304,8,256]{3,2,1,0:T(8,128)(2,1)}, bf16[1,2304,8,25...) fusion(bf16[6,2304,8,256]{3,2,1,0:T(8,128)(2,1)} %param.10), kind=kLoop, calls=%fused_computation.502 | loop fusion | bytes 113246208 | tf_op jit(solution)/shard_map/slice | solution.py:159
  106.8 9.1 fusion.300
  120.7 10.9 collective-permute-done.1
  138.8 5.8 fusion.299
  144.7 4.7 fusion.79
  151.5 6.0 fusion.298
  157.5 9.4 multiply_reduce_fusion.5
  167.9 6.1 fusion.348
  176.9 4.0 collective-permute-start.2
  181.0 4.6 collective-permute-start.3
  185.6 5.4 fusion.301
  191.1 33.9 %collective-permute-done.2 = bf16[2,512,4,256]{3,1,2,0:T(8,128)(2,1)S(1)} collective-permute-done((bf16[2,512,4,256]{3,1,2,0:T(8,128)(2,1)S(1)}, bf16[2,512,4,256]{3,1,2,0:T(8,128)(2,1)S(1)}, u32[]{:S(2)}, u32[]{:S(2)}) %collective-permute-start.2) | collective-permute-done | bytes 2097184 | tf_op jit(solution)/shard_map/ppermute | solution.py:54
  225.1 23.6 %collective-permute-done.3 = bf16[2,512,4,256]{3,1,2,0:T(8,128)(2,1)S(1)} collective-permute-done((bf16[2,512,4,256]{3,1,2,0:T(8,128)(2,1)S(1)}, bf16[2,512,4,256]{3,1,2,0:T(8,128)(2,1)S(1)}, u32[]{:S(2)}, u32[]{:S(2)}) %collective-permute-start.3) | collective-permute-done | bytes 2097184 | tf_op jit(solution)/shard_map/ppermute | solution.py:54
  252.2 4.1 fusion.81
  258.5 8.7 fusion.297
  269.3 5.9 fusion.296
  275.3 9.3 multiply_reduce_fusion.4
  285.6 6.1 fusion.350
  294.6 4.1 collective-permute-start.4
  298.7 4.6 collective-permute-start.5
  303.4 5.4 fusion.302
  308.9 33.8 %collective-permute-done.4 = bf16[2,512,4,256]{3,1,2,0:T(8,128)(2,1)S(1)} collective-permute-done((bf16[2,512,4,256]{3,1,2,0:T(8,128)(2,1)S(1)}, bf16[2,512,4,256]{3,1,2,0:T(8,128)(2,1)S(1)}, u32[]{:S(2)}, u32[]{:S(2)}) %collective-permute-start.4) | collective-permute-done | bytes 2097184 | tf_op jit(solution)/shard_map/ppermute | solution.py:54
  342.9 23.6 %collective-permute-done.5 = bf16[2,512,4,256]{3,1,2,0:T(8,128)(2,1)S(1)} collective-permute-done((bf16[2,512,4,256]{3,1,2,0:T(8,128)(2,1)S(1)}, bf16[2,512,4,256]{3,1,2,0:T(8,128)(2,1)S(1)}, u32[]{:S(2)}, u32[]{:S(2)}) %collective-permute-start.5) | collective-permute-done | bytes 2097184 | tf_op jit(solution)/shard_map/ppermute | solution.py:54
  369.9 4.0 fusion.83
  376.1 8.8 fusion.295
  387.0 6.0 fusion.294
  393.0 9.3 multiply_reduce_fusion.3
  403.3 6.1 fusion.352
  412.3 5.3 collective-permute-start.6
  417.6 4.6 collective-permute-start.7
  422.2 5.4 fusion.303
  427.8 35.1 %collective-permute-done.6 = bf16[2,512,4,256]{3,1,2,0:T(8,128)(2,1)S(1)} collective-permute-done((bf16[2,512,4,256]{3,1,2,0:T(8,128)(2,1)S(1)}, bf16[2,512,4,256]{3,1,2,0:T(8,128)(2,1)S(1)}, u32[]{:S(2)}, u32[]{:S(2)}) %collective-permute-start.6) | collective-permute-done | bytes 2097184 | tf_op jit(solution)/shard_map/ppermute | solution.py:54
  463.0 22.4 %collective-permute-done.7 = bf16[2,512,4,256]{3,1,2,0:T(8,128)(2,1)S(1)} collective-permute-done((bf16[2,512,4,256]{3,1,2,0:T(8,128)(2,1)S(1)}, bf16[2,512,4,256]{3,1,2,0:T(8,128)(2,1)S(1)}, u32[]{:S(2)}, u32[]{:S(2)}) %collective-permute-start.7) | collective-permute-done | bytes 2097184 | tf_op jit(solution)/shard_map/ppermute | solution.py:54
  488.8 4.1 fusion.85
  495.0 8.7 fusion.293
  505.9 6.0 fusion.292
  511.9 9.3 multiply_reduce_fusion.2
  522.2 6.1 fusion.354
  534.3 4.6 collective-permute-start.9
  539.0 5.4 fusion.304
  544.5 32.9 %collective-permute-done.8 = bf16[2,512,4,256]{3,1,2,0:T(8,128)(2,1)S(1)} collective-permute-done((bf16[2,512,4,256]{3,1,2,0:T(8,128)(2,1)S(1)}, bf16[2,512,4,256]{3,1,2,0:T(8,128)(2,1)S(1)}, u32[]{:S(2)}, u32[]{:S(2)}) %collective-permute-start.8) | collective-permute-done | bytes 2097184 | tf_op jit(solution)/shard_map/ppermute | solution.py:54
  577.6 24.5 %collective-permute-done.9 = bf16[2,512,4,256]{3,1,2,0:T(8,128)(2,1)S(1)} collective-permute-done((bf16[2,512,4,256]{3,1,2,0:T(8,128)(2,1)S(1)}, bf16[2,512,4,256]{3,1,2,0:T(8,128)(2,1)S(1)}, u32[]{:S(2)}, u32[]{:S(2)}) %collective-permute-start.9) | collective-permute-done | bytes 2097184 | tf_op jit(solution)/shard_map/ppermute | solution.py:54
  611.8 8.8 fusion.291
  622.7 5.9 fusion.290
  628.6 9.6 multiply_reduce_fusion.1
  639.0 4.4 collective-permute-start.10
  647.0 47.9 %collective-permute-done.10 = bf16[256,2304]{1,0:T(8,128)(2,1)S(1)} collective-permute-done((bf16[256,2304]{1,0:T(8,128)(2,1)S(1)}, bf16[256,2304]{1,0:T(8,128)(2,1)S(1)}, u32[]{:S(2)}, u32[]{:S(2)}) %collective-permute-start.10) | collective-permute-done | bytes 1179680 | tf_op jit(solution)/shard_map/ppermute | solution.py:88
  695.0 25.8 %collective-permute-done.11 = bf16[256,2304]{1,0:T(8,128)(2,1)} collective-permute-done((bf16[256,2304]{1,0:T(8,128)(2,1)S(1)}, bf16[256,2304]{1,0:T(8,128)(2,1)}, u32[]{:S(2)}, u32[]{:S(2)}) %collective-permute-start.11) | collective-permute-done | bytes 1179680 | tf_op jit(solution)/shard_map/ppermute | solution.py:89
  722.9 5.3 fusion.359
  732.4 7.9 fusion.305
  741.5 182.1 %all-gather.3.cloned.1.call-done = bf16[32,512,4,256]{3,1,2,0:T(8,128)(2,1)} async-done(((bf16[2,512,4,256]{3,1,2,0:T(8,128)(2,1)}), bf16[32,512,4,256]{3,1,2,0:T(8,128)(2,1)}) %all-gather.3.cloned.1.call-update) | async-done | bytes 33554448 | tf_op jit(solution)/shard_map/all_gather | solution.py:139
  923.5 23.1 %copy.68 = bf16[16,2,2,256,4,256]{5,3,4,2,1,0:T(8,128)(2,1)} copy(bf16[16,2,2,256,4,256]{5,3,2,4,1,0:T(8,128)(2,1)} %bitcast.669) | data formatting | bytes 67108864
  948.1 13.2 %while.30 = (s32[]{:T(128)}, f32[4,2,256]{2,1,0:T(2,128)S(1)}, f32[4,2,256]{2,1,0:T(2,128)S(1)}, f32[4,2,256,256]{3,2,1,0:T(8,128)}, s32[]{:T(128)}, /*index=5*/...) while((s32[]{:T(128)}, f32[4,2,256]{2,1,0:T(2,128)S(1)}, ...), condition=%wide.region_34.35_spmd.clone, body=%wide.region_31.34_spmd.clone.sunk | while | flops 544870912 | bytes 12980490 | solution.py:129
  962.8 194.1 %while.31 = (s32[]{:T(128)}, f32[4,2,256]{2,1,0:T(2,128)S(1)}, f32[4,2,256]{2,1,0:T(2,128)S(1)}, f32[4,2,256,256]{3,2,1,0:T(8,128)}, s32[]{:T(128)}, /*index=5*/...) while((s32[]{:T(128)}, f32[4,2,256]{2,1,0:T(2,128)S(1)}, ...), condition=%wide.region_38.39_spmd.clone, body=%wide.region_35.38_spmd.clone.sunk | while | flops 544870912 | bytes 12980490 | solution.py:129
  965.0 4.0 multiply_add_fusion.11
  977.5 4.0 multiply_add_fusion.11
  1021.3 4.0 multiply_add_fusion.11
  1033.9 4.0 multiply_add_fusion.11
  1077.7 4.0 multiply_add_fusion.11
  1159.4 8.6 multiply_reduce_fusion
  (471 shorter events, 285.5 us)
Async XLA Ops:
  6.5 917.0 %all-gather.3.cloned.1.call-start = ((), (), s32[]{:S(2)}) async-start(), calls=%async_computation | async-start | bytes 35651584 | tf_op jit(solution)/shard_map/all_gather | solution.py:139
  6.6 28.3 %copy-start.1 = (bf16[6,2304,4,256]{3,2,1,0:T(4,128)(2,1)S(1)}, bf16[6,2304,4,256]{3,2,1,0:T(4,128)(2,1)}, u32[]{:S(2)}) copy-start(bf16[6,2304,4,256]{3,2,1,0:T(4,128)(2,1)} %param.12) | copy-start | bytes 84934656
  48.1 5.9 copy-start.12
  48.1 5.9 copy-start.20
  53.9 2.7 copy-start.23
  59.1 59.8 %collective-permute-start = (bf16[2,512,4,256]{3,1,2,0:T(8,128)(2,1)}, bf16[2,512,4,256]{3,1,2,0:T(8,128)(2,1)}, u32[]{:S(2)}, u32[]{:S(2)}) collective-permute-start(bf16[2,512,4,256]{3,1,2,0:T(8,128)(2,1)} %pad_maximum_fusion.11), channel_id=1, source_target_pairs={{0,2},{1,3},{2,4},{3,5},{4,6},{5,7},{6,8},{7,9},{8,10},{9,11},{10,... | collective-permute-start | bytes 6291464 | tf_op jit(solution)/shard_map/ppermute | solution.py:54
  65.0 66.6 %collective-permute-start.1 = (bf16[2,512,4,256]{3,1,2,0:T(8,128)(2,1)}, bf16[2,512,4,256]{3,1,2,0:T(8,128)(2,1)}, u32[]{:S(2)}, u32[]{:S(2)}) collective-permute-start(bf16[2,512,4,256]{3,1,2,0:T(8,128)(2,1)} %pad_maximum_fusion.11), channel_id=1, source_target_pairs={{0,1},{1,2},{2,3},{3,4},{4,5},{5,6},{6,7},{7,8},{8,9},{9,10},{10,1... | collective-permute-start | bytes 6291464 | tf_op jit(solution)/shard_map/ppermute | solution.py:54
  157.5 9.4 copy-start.13
  166.9 7.2 slice-start.20
  167.9 17.7 %copy-start.18 = (bf16[512,2304]{1,0:T(8,128)(2,1)}, bf16[512,2304]{1,0:T(8,128)(2,1)S(1)}, u32[]{:S(2)}) copy-start(bf16[512,2304]{1,0:T(8,128)(2,1)S(1)} %get-tuple-element.212) | copy-start | bytes 7077892
  167.9 6.1 slice-start.21
  174.0 76.5 %copy-start.29 = (bf16[512,4,256]{2,0,1:T(8,128)(2,1)}, bf16[512,4,256]{2,0,1:T(8,128)(2,1)S(1)}, u32[]{:S(2)}) copy-start(bf16[512,4,256]{2,0,1:T(8,128)(2,1)S(1)} %fusion.348) | copy-start | bytes 3145732
  174.0 11.6 slice-start.9
  174.0 11.5 slice-start.10
  174.1 11.5 slice-start.11
  176.7 8.8 copy-start.26
  176.9 48.1 %collective-permute-start.2 = (bf16[2,512,4,256]{3,1,2,0:T(8,128)(2,1)S(1)}, bf16[2,512,4,256]{3,1,2,0:T(8,128)(2,1)S(1)}, u32[]{:S(2)}, u32[]{:S(2)}) collective-permute-start(bf16[2,512,4,256]{3,1,2,0:T(8,128)(2,1)S(1)} %pad_maximum_fusion.12), channel_id=1, source_target_pairs={{0,2},{1,3},{2,4},{3,5},{4,6},{5,7},{6,8},{7,9},{8,10},{9,11},{10,... | collective-permute-start | bytes 6291464 | tf_op jit(solution)/shard_map/ppermute | solution.py:54
  181.0 67.7 %collective-permute-start.3 = (bf16[2,512,4,256]{3,1,2,0:T(8,128)(2,1)S(1)}, bf16[2,512,4,256]{3,1,2,0:T(8,128)(2,1)S(1)}, u32[]{:S(2)}, u32[]{:S(2)}) collective-permute-start(bf16[2,512,4,256]{3,1,2,0:T(8,128)(2,1)S(1)} %pad_maximum_fusion.12), channel_id=1, source_target_pairs={{0,1},{1,2},{2,3},{3,4},{4,5},{5,6},{6,7},{7,8},{8,9},{9,10},{10,1... | collective-permute-start | bytes 6291464 | tf_op jit(solution)/shard_map/ppermute | solution.py:54
  252.2 4.1 copy-start.7
  275.3 9.3 copy-start.19
  284.6 7.1 slice-start.18
  285.6 17.7 %copy-start.14 = (bf16[512,2304]{1,0:T(8,128)(2,1)}, bf16[512,2304]{1,0:T(8,128)(2,1)S(1)}, u32[]{:S(2)}) copy-start(bf16[512,2304]{1,0:T(8,128)(2,1)S(1)} %get-tuple-element.210) | copy-start | bytes 7077892
  285.6 6.1 slice-start.19
  291.7 76.4 %copy-start.30 = (bf16[512,4,256]{2,0,1:T(8,128)(2,1)}, bf16[512,4,256]{2,0,1:T(8,128)(2,1)S(1)}, u32[]{:S(2)}) copy-start(bf16[512,4,256]{2,0,1:T(8,128)(2,1)S(1)} %fusion.350) | copy-start | bytes 3145732
  291.7 11.6 slice-start.6
  291.7 11.6 slice-start.7
  291.8 11.6 slice-start.8
  294.4 8.9 copy-start.27
  294.6 48.1 %collective-permute-start.4 = (bf16[2,512,4,256]{3,1,2,0:T(8,128)(2,1)S(1)}, bf16[2,512,4,256]{3,1,2,0:T(8,128)(2,1)S(1)}, u32[]{:S(2)}, u32[]{:S(2)}) collective-permute-start(bf16[2,512,4,256]{3,1,2,0:T(8,128)(2,1)S(1)} %pad_maximum_fusion.13), channel_id=1, source_target_pairs={{0,2},{1,3},{2,4},{3,5},{4,6},{5,7},{6,8},{7,9},{8,10},{9,11},{10,... | collective-permute-start | bytes 6291464 | tf_op jit(solution)/shard_map/ppermute | solution.py:54
  298.7 67.7 %collective-permute-start.5 = (bf16[2,512,4,256]{3,1,2,0:T(8,128)(2,1)S(1)}, bf16[2,512,4,256]{3,1,2,0:T(8,128)(2,1)S(1)}, u32[]{:S(2)}, u32[]{:S(2)}) collective-permute-start(bf16[2,512,4,256]{3,1,2,0:T(8,128)(2,1)S(1)} %pad_maximum_fusion.13), channel_id=1, source_target_pairs={{0,1},{1,2},{2,3},{3,4},{4,5},{5,6},{6,7},{7,8},{8,9},{9,10},{10,1... | collective-permute-start | bytes 6291464 | tf_op jit(solution)/shard_map/ppermute | solution.py:54
  369.9 4.1 copy-start.8
  393.0 9.3 copy-start.15
  402.3 7.1 slice-start.16
  403.3 18.9 %copy-start.16 = (bf16[512,2304]{1,0:T(8,128)(2,1)}, bf16[512,2304]{1,0:T(8,128)(2,1)S(1)}, u32[]{:S(2)}) copy-start(bf16[512,2304]{1,0:T(8,128)(2,1)S(1)} %get-tuple-element.208) | copy-start | bytes 7077892
  403.3 6.1 slice-start.17
  409.4 77.7 %copy-start.31 = (bf16[512,4,256]{2,0,1:T(8,128)(2,1)}, bf16[512,4,256]{2,0,1:T(8,128)(2,1)S(1)}, u32[]{:S(2)}) copy-start(bf16[512,4,256]{2,0,1:T(8,128)(2,1)S(1)} %fusion.352) | copy-start | bytes 3145732
  409.4 12.8 %slice-start.3 = ((s8[9437184]{0:T(1024)(128)(4,1)}), s8[4194304]{0:T(1024)(128)(4,1)S(1)}, s32[]{:S(2)}) async-start(s8[9437184]{0:T(1024)(128)(4,1)} %bitcast.672), calls=%async_computation.4 | async-start | bytes 8388608
  409.4 12.8 %slice-start.4 = ((s8[9437184]{0:T(1024)(128)(4,1)}), s8[4194304]{0:T(1024)(128)(4,1)S(1)}, s32[]{:S(2)}) async-start(s8[9437184]{0:T(1024)(128)(4,1)} %bitcast.672), calls=%async_computation.5 | async-start | bytes 8388608
  409.4 12.8 %slice-start.5 = ((s8[9437184]{0:T(1024)(128)(4,1)}), s8[1048576]{0:T(1024)(128)(4,1)S(1)}, s32[]{:S(2)}) async-start(s8[9437184]{0:T(1024)(128)(4,1)} %bitcast.672), calls=%async_computation.6 | async-start | bytes 2097152
  412.1 10.1 copy-start.28
  412.3 50.5 %collective-permute-start.6 = (bf16[2,512,4,256]{3,1,2,0:T(8,128)(2,1)S(1)}, bf16[2,512,4,256]{3,1,2,0:T(8,128)(2,1)S(1)}, u32[]{:S(2)}, u32[]{:S(2)}) collective-permute-start(bf16[2,512,4,256]{3,1,2,0:T(8,128)(2,1)S(1)} %pad_maximum_fusion.14), channel_id=1, source_target_pairs={{0,2},{1,3},{2,4},{3,5},{4,6},{5,7},{6,8},{7,9},{8,10},{9,11},{10,... | collective-permute-start | bytes 6291464 | tf_op jit(solution)/shard_map/ppermute | solution.py:54
  417.6 67.7 %collective-permute-start.7 = (bf16[2,512,4,256]{3,1,2,0:T(8,128)(2,1)S(1)}, bf16[2,512,4,256]{3,1,2,0:T(8,128)(2,1)S(1)}, u32[]{:S(2)}, u32[]{:S(2)}) collective-permute-start(bf16[2,512,4,256]{3,1,2,0:T(8,128)(2,1)S(1)} %pad_maximum_fusion.14), channel_id=1, source_target_pairs={{0,1},{1,2},{2,3},{3,4},{4,5},{5,6},{6,7},{7,8},{8,9},{9,10},{10,1... | collective-permute-start | bytes 6291464 | tf_op jit(solution)/shard_map/ppermute | solution.py:54
  488.8 4.1 copy-start.9
  511.8 9.3 copy-start.17
  521.2 7.1 slice-start.14
  522.2 16.8 %copy-start.10 = (bf16[512,2304]{1,0:T(8,128)(2,1)}, bf16[512,2304]{1,0:T(8,128)(2,1)S(1)}, u32[]{:S(2)}) copy-start(bf16[512,2304]{1,0:T(8,128)(2,1)S(1)} %get-tuple-element.206) | copy-start | bytes 7077892
  522.2 6.1 slice-start.15
  528.3 75.6 %copy-start.32 = (bf16[512,4,256]{2,0,1:T(8,128)(2,1)}, bf16[512,4,256]{2,0,1:T(8,128)(2,1)S(1)}, u32[]{:S(2)}) copy-start(bf16[512,4,256]{2,0,1:T(8,128)(2,1)S(1)} %fusion.354) | copy-start | bytes 3145732
  528.3 10.7 slice-start
  528.3 10.7 slice-start.1
  528.3 10.7 slice-start.2
  531.0 8.0 copy-start.25
  531.2 46.2 %collective-permute-start.8 = (bf16[2,512,4,256]{3,1,2,0:T(8,128)(2,1)S(1)}, bf16[2,512,4,256]{3,1,2,0:T(8,128)(2,1)S(1)}, u32[]{:S(2)}, u32[]{:S(2)}) collective-permute-start(bf16[2,512,4,256]{3,1,2,0:T(8,128)(2,1)S(1)} %pad_maximum_fusion.15), channel_id=1, source_target_pairs={{0,2},{1,3},{2,4},{3,5},{4,6},{5,7},{6,8},{7,9},{8,10},{9,11},{10,... | collective-permute-start | bytes 6291464 | tf_op jit(solution)/shard_map/ppermute | solution.py:54
  534.3 67.7 %collective-permute-start.9 = (bf16[2,512,4,256]{3,1,2,0:T(8,128)(2,1)S(1)}, bf16[2,512,4,256]{3,1,2,0:T(8,128)(2,1)S(1)}, u32[]{:S(2)}, u32[]{:S(2)}) collective-permute-start(bf16[2,512,4,256]{3,1,2,0:T(8,128)(2,1)S(1)} %pad_maximum_fusion.15), channel_id=1, source_target_pairs={{0,1},{1,2},{2,3},{3,4},{4,5},{5,6},{6,7},{7,8},{8,9},{9,10},{10,1... | collective-permute-start | bytes 6291464 | tf_op jit(solution)/shard_map/ppermute | solution.py:54
  605.6 4.0 copy-start.6
  628.6 9.6 copy-start.11
  639.0 56.0 %collective-permute-start.10 = (bf16[256,2304]{1,0:T(8,128)(2,1)S(1)}, bf16[256,2304]{1,0:T(8,128)(2,1)S(1)}, u32[]{:S(2)}, u32[]{:S(2)}) collective-permute-start(bf16[256,2304]{1,0:T(8,128)(2,1)S(1)} %get-tuple-element.251), channel_id=1, source_target_pairs={{0,0},{1,2},{2,4},{3,6},{4,8},{5,10},{6,12},{7,14},{8,15},{9,13},{... | collective-permute-start | bytes 3538952 | tf_op jit(solution)/shard_map/ppermute | solution.py:88
  643.5 77.3 %collective-permute-start.11 = (bf16[256,2304]{1,0:T(8,128)(2,1)S(1)}, bf16[256,2304]{1,0:T(8,128)(2,1)}, u32[]{:S(2)}, u32[]{:S(2)}) collective-permute-start(bf16[256,2304]{1,0:T(8,128)(2,1)S(1)} %get-tuple-element.252), channel_id=1, source_target_pairs={{0,1},{1,3},{2,5},{3,7},{4,9},{5,11},{6,13},{7,15},{8,14},{9,12},{... | collective-permute-start | bytes 3538952 | tf_op jit(solution)/shard_map/ppermute | solution.py:89
  720.7 7.4 slice-start.12
  722.3 10.1 copy-start.2
  722.3 10.1 copy-start.4
  722.9 5.3 slice-start.13
  1159.4 8.7 copy-start.3
  1159.4 8.7 copy-start.5
  (4 other events, 6.6 us)
Sparse Core Ops, SparseCore 0:
  732.5 190.9 all-gather.2
where the time goes:
time: 1190 us; the launch traced here: 1180 us
  waiting for transfers between devices  496 us (42%)
  matrix products  429 us (36%)
  local copies, waits for them, and re-layouts  120 us (10%)
  other arithmetic  62.9 us (5%)
  starting transfers between devices  52 us (4%)
  between operations  15 us (1%)
    ppermute x10, waiting for transfers between devices, gather_halo(): pieces.append(lax.ppermute(tail_kv, 'cp', perm_pairs))  241 us
    all_gather x1, waiting for transfers between devices, global_layer(): kv_all = lax.all_gather(jnp.stack([key_rows, value_rows]), 'cp')  182 us
    dot_general x33, matrix products, kv_step(): jnp.einsum('hgqk,khd->hgqd', weights.astype(jnp.bfloat16), kv_block[1], p...  133 us
    dot_general x10, matrix products, window_attention(): jnp.einsum('hgqk,khd->hgqd', weights.astype(jnp.bfloat16), value_rows, pr...  70.5 us
    dot_general x6, matrix products, residual_update(): jnp.einsum('the,hed->td', attn_out, w_out, preferred_element_type=jnp.flo...  55.4 us
    dot_general x33, matrix products, kv_step(): jnp.einsum('qhgd,khd->hgqk', grouped, kv_block[0], preferred_element_type...  51.7 us
    ppermute x1, waiting for transfers between devices, to_output_layout(): from_even = lax.ppermute(hidden[:block_len], 'cp', even_pairs)  47.9 us
    ppermute x10, starting transfers between devices, gather_halo(): pieces.append(lax.ppermute(tail_kv, 'cp', perm_pairs))  44 us
  transfers between devices with their start and end apart: 13, of which 12 were waited for; matrix products, arithmetic and copies ran while one was open for 7% of the time, Pallas kernels for 0%

commit v1 on v0

v1 whole, which is shorter than its diff:
```python
import functools

import jax
import jax.numpy as jnp
from jax import lax
from jax.experimental import pallas as pl
from jax.experimental.pallas import tpu as pltpu
from jax.sharding import PartitionSpec as P

WINDOW = 1024
EPS_NORM = 1e-6
NEG_BIG = -1e30
LOG2_E = 1.4426950408889634
BLK = 256
VMEM_BYTES = 62 << 20


def params(**kw):
    return pltpu.CompilerParams(vmem_limit_bytes=VMEM_BYTES, **kw)


def normed(rows):
    wide = rows.astype(jnp.float32)
    return (wide * lax.rsqrt(jnp.mean(wide * wide, axis=-1, keepdims=True) + EPS_NORM)).astype(jnp.bfloat16)


def proj_kernel(layer, num_w, num_parts, *refs):
    x_ref, refs = refs[0], refs[1:]
    w_hbm, outs, n_s = refs[:num_w], refs[num_w:2 * num_w], refs[2 * num_w]
    stages, flats = refs[2 * num_w + 1:3 * num_w + 1], refs[3 * num_w + 1:4 * num_w + 1]
    sems = refs[-1]
    dim = x_ref.shape[1]
    part = dim // num_parts
    copies = []
    for i in range(num_w):
        row = []
        for p in range(num_parts):
            cp = pltpu.make_async_copy(w_hbm[i].at[layer, pl.ds(p * part, part)], stages[i].at[pl.ds(p * part, part)], sems.at[i, p])
            cp.start()
            row.append(cp)
        copies.append(row)
    n_s[...] = normed(x_ref[...])

    def flatten(i, start, size):
        rows = pl.ds(start, size)
        flats[i][rows, :] = stages[i][rows].reshape(size, -1)

    for p in range(num_parts):
        copies[0][p].wait()
        for b in range(0, part, BLK):
            flatten(0, p * part + b, BLK)
    for i in range(num_w):
        more = list(range(i + 1, num_w)) if i == 0 else []
        for j in more:
            for p in range(num_parts):
                copies[j][p].wait()
        width = flats[i].shape[1]
        tile = 512
        steps = width // tile
        rows = dim // steps

        @pl.loop(0, steps)
        def _(s):
            for j in more:
                flatten(j, pl.multiple_of(s * rows, 16), rows)
            cols = pl.ds(pl.multiple_of(s * tile, tile), tile)
            outs[i][:, cols] = jnp.dot(n_s[...], flats[i][:, cols], preferred_element_type=jnp.float32).astype(jnp.bfloat16)


def project(x, weights, layer):
    rows, dim = x.shape
    num_parts = 3
    shapes = [w.shape[2:] for w in weights]
    widths = [h * e for h, e in shapes]
    num_w = len(weights)
    vm = pl.BlockSpec(memory_space=pltpu.VMEM)
    flops = 2 * rows * dim * sum(widths)
    return pl.pallas_call(
        functools.partial(proj_kernel, layer, num_w, num_parts),
        in_specs=[vm] + [pl.BlockSpec(memory_space=pl.ANY)] * num_w,
        out_specs=[vm] * num_w,
        out_shape=[jax.ShapeDtypeStruct((rows, n), jnp.bfloat16) for n in widths],
        scratch_shapes=[pltpu.VMEM((rows, dim), jnp.bfloat16)]
        + [pltpu.VMEM((dim,) + s, jnp.bfloat16) for s in shapes]
        + [pltpu.VMEM((dim, n), jnp.bfloat16) for n in widths]
        + [pltpu.SemaphoreType.DMA((num_w, num_parts))],
        compiler_params=params(),
        cost_estimate=pl.CostEstimate(flops=flops, bytes_accessed=2 * dim * sum(widths), transcendentals=0),
        name=f"proj{num_w}",
    )(x, *weights)


def output_rows(o_s, w_s, x_ref, out_ref, upd_s):
    rows, dim = x_ref.shape
    tile = 768

    @pl.loop(0, dim // tile)
    def _(s):
        cols = pl.ds(pl.multiple_of(s * tile, tile), tile)
        upd_s[:, cols] = jnp.dot(o_s[...], w_s[:, cols], preferred_element_type=jnp.float32)

    @pl.loop(0, rows // 64)
    def _(s):
        part = pl.ds(pl.multiple_of(s * 64, 64), 64)
        upd = upd_s[part, :]
        scale = lax.rsqrt(jnp.mean(upd * upd, axis=-1, keepdims=True) + EPS_NORM)
        out_ref[part, :] = (x_ref[part, :].astype(jnp.float32) + upd * scale).astype(jnp.bfloat16)


def soft_block(q, keys, values, kinds):
    scores = []
    for k, kind in zip(keys, kinds):
        s = lax.dot_general(q, k, (((1,), (1,)), ((), ())), preferred_element_type=jnp.float32)
        if kind:
            qi = lax.broadcasted_iota(jnp.int32, s.shape, 0)
            ki = lax.broadcasted_iota(jnp.int32, s.shape, 1)
            s = jnp.where(ki <= qi if kind == 1 else ki > qi, s, NEG_BIG)
        scores.append(s)
    top = jnp.max(functools.reduce(jnp.maximum, scores), axis=-1, keepdims=True)
    factor = LOG2_E * q.shape[-1] ** -0.5
    acc = total = None
    for s, v in zip(scores, values):
        e = jnp.exp2((s - top) * factor)
        d = jnp.dot(e.astype(jnp.bfloat16), v, preferred_element_type=jnp.float32)
        total = e if total is None else total + e
        acc = d if acc is None else acc + d
    return (acc / jnp.sum(total, axis=-1, keepdims=True)).astype(jnp.bfloat16)


def window_kernel(layer, c_ref, q_ref, *refs):
    keys, values, (x_ref, w_hbm, out_ref, o_s, w_s, upd_s, sem) = refs[0:6:2], refs[1:6:2], refs[6:]
    g = pl.program_id(0)
    c = c_ref[0]
    wcopy = pltpu.make_async_copy(w_hbm.at[layer], w_s, sem)

    @pl.when(g == 0)
    def _():
        wcopy.start()

    def run(first_chunk):
        kinds = [-1, 0, 0, 0, 1]
        for i in range(2):
            picks = [(i + j, kinds[j]) for j in range(5) if (i + j) // 2 >= first_chunk]
            ks = [keys[b // 2][(b % 2) * BLK:(b % 2 + 1) * BLK, :] for b, _ in picks]
            vs = [values[b // 2][(b % 2) * BLK:(b % 2 + 1) * BLK, :] for b, _ in picks]
            for h in range(2):
                q = q_ref[i * BLK:(i + 1) * BLK, h * BLK:(h + 1) * BLK]
                res = soft_block(q, ks, vs, [kind for _, kind in picks])
                o_s[i * BLK:(i + 1) * BLK, pl.ds(pl.multiple_of(g * 2 * BLK + h * BLK, BLK), BLK)] = res

    for first, cond in ((0, c >= 2), (1, c == 1), (2, c == 0)):
        @pl.when(cond)
        def _():
            run(first)

    @pl.when(g == pl.num_programs(0) - 1)
    def _():
        wcopy.wait()
        output_rows(o_s, w_s, x_ref, out_ref, upd_s)


def window_layer(chunk, q, kvs, x, w_out, layer):
    rows, dim = x.shape
    kv = pl.BlockSpec((rows, BLK), lambda g, c: (0, g))
    row = pl.BlockSpec((rows, dim), lambda g, c: (0, 0))
    return pl.pallas_call(
        functools.partial(window_kernel, layer),
        grid_spec=pltpu.PrefetchScalarGridSpec(
            num_scalar_prefetch=1,
            grid=(kvs[0].shape[1] // BLK,),
            in_specs=[pl.BlockSpec((rows, 2 * BLK), lambda g, c: (0, g))] + [kv] * 6 + [row, pl.BlockSpec(memory_space=pl.ANY)],
            out_specs=row,
            scratch_shapes=[
                pltpu.VMEM(q.shape, jnp.bfloat16),
                pltpu.VMEM(w_out.shape[1:], jnp.bfloat16),
                pltpu.VMEM((rows, dim), jnp.float32),
                pltpu.SemaphoreType.DMA,
            ],
        ),
        out_shape=jax.ShapeDtypeStruct((rows, dim), jnp.bfloat16),
        compiler_params=params(),
        cost_estimate=pl.CostEstimate(flops=15 * 10 ** 9, bytes_accessed=2 * w_out[0].size, transcendentals=0),
        name="window",
    )(chunk, q, *kvs, x, w_out)


MESH = pl.DeviceIdType.MESH


def gather_kernel(num_dev, layer, shift, x_hbm, wk_hbm, wv_hbm, k_all, v_all, x_all,
                  wk_st, wv_st, wk_s, wv_s, x_s, n_s, k_s, v_s, wsem, lsem, ssem, send, recv, psend, precv):
    rows, dim = x_s.shape
    half = rows // 2
    me = lax.axis_index("cp")
    other = me + 1 - 2 * lax.rem(me, 2)
    near = (lax.rem(me + 2, num_dev), lax.rem(me + num_dev - 2, num_dev))
    hops = num_dev // 4

    def wrap(v):
        return lax.rem(v + 4 * num_dev, num_dev)

    def owner(dev, way, hop):
        return wrap(dev - 2 * hop) if way == 0 else wrap(dev + 2 * hop)

    def piece(dev, h):
        return x_all.at[dev, pl.ds(h * half, half)]

    def link(way, hop, h):
        ref = piece(owner(me, way, hop - 1), h)
        return pltpu.make_async_remote_copy(src_ref=ref, dst_ref=ref, send_sem=send.at[way, hop, h], recv_sem=recv.at[way, hop, h],
                                            device_id={"cp": near[way]}, device_id_type=MESH)

    def landed(way, hop, h):
        ref = piece(owner(me, way, hop), h)
        return pltpu.make_async_remote_copy(src_ref=ref, dst_ref=ref, send_sem=send.at[way, hop, h], recv_sem=recv.at[way, hop, h],
                                            device_id={"cp": near[way]}, device_id_type=MESH)

    def across(way, hop, h, dev):
        ref = piece(owner(dev, way, hop), h)
        return pltpu.make_async_remote_copy(src_ref=ref, dst_ref=ref, send_sem=psend.at[way, hop, h], recv_sem=precv.at[way, hop, h],
                                            device_id={"cp": other}, device_id_type=MESH)

    wcopies = [pltpu.make_async_copy(w.at[layer], st, wsem.at[i]) for i, (w, st) in enumerate(((wk_hbm, wk_st), (wv_hbm, wv_st)))]
    for cp in wcopies:
        cp.start()
    first = pltpu.make_async_copy(x_hbm, x_s, lsem)
    first.start()
    barrier = pltpu.get_barrier_semaphore()
    for dev in near + (other,):
        pl.semaphore_signal(barrier, inc=1, device_id={"cp": dev}, device_id_type=MESH)
    pl.semaphore_wait(barrier, 3)
    first.wait()
    keep = pltpu.make_async_copy(x_s, x_all.at[me], lsem)
    keep.start()
    keep.wait()
    for h in range(2):
        for way in range(2):
            link(way, 1, h).start()
    for h in range(2):
        across(0, 0, h, me).start()
    for cp in wcopies:
        cp.wait()
    step_rows = 256

    @pl.loop(0, dim // step_rows)
    def _(s):
        part = pl.ds(pl.multiple_of(s * step_rows, step_rows), step_rows)
        wk_s[part, :] = wk_st[part].reshape(step_rows, -1)
        wv_s[part, :] = wv_st[part].reshape(step_rows, -1)

    @pl.loop(0, hops + 1)
    def _(hop):
        for h in range(2):
            for way in range(2):
                last_ok = way == h

                def arrive():
                    landed(way, hop, h).wait_recv()
                    if last_ok:
                        @pl.when(hop < hops)
                        def _():
                            link(way, hop + 1, h).start()
                    else:
                        @pl.when(hop < hops - 1)
                        def _():
                            link(way, hop + 1, h).start()
                    across(way, hop, h, me).start()

                if last_ok:
                    pl.when(hop > 0)(arrive)
                else:
                    pl.when((hop > 0) & (hop < hops))(arrive)

        whole = (hop > 0) & (hop < hops)

        @pl.loop(0, 4)
        def _(a):
            way = lax.rem(a, 2)
            mine = a < 2

            @pl.when(whole | (way == 0))
            def _():
                @pl.when(jnp.logical_not(mine))
                def _():
                    for w in range(2):
                        for h in range(2):
                            pair = ((hop > 0) & (hop < hops) & (way == w))
                            if w == 0:
                                pair = pair | (hop == 0)
                            if w == h:
                                pair = pair | (hop == hops)

                            @pl.when(pair)
                            def _():
                                across(w, hop, h, other).wait_recv()

                dev = jnp.where(mine, me, other)
                src = wrap(dev + jnp.where(way == 0, -2, 2) * hop)
                load = pltpu.make_async_copy(x_all.at[src], x_s, lsem)
                load.start()
                load.wait()
                n_s[...] = normed(x_s[...])
                k_s[...] = jnp.dot(n_s[...], wk_s[...], preferred_element_type=jnp.float32).astype(jnp.bfloat16)
                v_s[...] = jnp.dot(n_s[...], wv_s[...], preferred_element_type=jnp.float32).astype(jnp.bfloat16)
                chunk = wrap(src + shift)
                stores = [pltpu.make_async_copy(s, o.at[chunk], ssem.at[i]) for i, (s, o) in enumerate(((k_s, k_all), (v_s, v_all)))]
                for cp in stores:
                    cp.start()
                for cp in stores:
                    cp.wait()

    for way in range(2):
        for hop in range(1, hops + 1):
            for h in range(2):
                if hop < hops or way == h:
                    link(way, hop, h).wait_send()
                    across(way, hop, h, me).wait_send()
    for h in range(2):
        across(0, 0, h, me).wait_send()


def gather_keys(x, w_key, w_value, layer, shift, num_dev):
    rows, dim = x.shape
    heads, head_dim = w_key.shape[2:]
    width = heads * head_dim
    hops = num_dev // 4
    any_ = pl.BlockSpec(memory_space=pl.ANY)
    bf = jnp.bfloat16
    sem = pltpu.SemaphoreType.DMA
    return pl.pallas_call(
        functools.partial(gather_kernel, num_dev, layer, shift),
        in_specs=[any_] * 3,
        out_specs=[any_] * 3,
        out_shape=[jax.ShapeDtypeStruct((num_dev, rows, n), bf) for n in (width, width, dim)],
        scratch_shapes=[pltpu.VMEM((dim, heads, head_dim), bf)] * 2 + [pltpu.VMEM((dim, width), bf)] * 2
        + [pltpu.VMEM((rows, dim), bf)] * 2 + [pltpu.VMEM((rows, width), bf)] * 2
        + [sem((2,)), sem, sem((2,))] + [sem((2, hops + 1, 2))] * 4,
        compiler_params=params(collective_id=1, has_side_effects=True),
        cost_estimate=pl.CostEstimate(flops=4 * rows * num_dev * dim * width, bytes_accessed=4 * dim * width, transcendentals=0),
        name="gather",
    )(x, w_key, w_value)


def causal_kernel(layer, seq, blk_ref, q_ref, k_ref, v_ref, x_ref, w_hbm, out_ref, o_s, w_s, upd_s, acc_s, top_s, tot_s, sem):
    g = pl.program_id(0)
    wcopy = pltpu.make_async_copy(w_hbm.at[layer], w_s, sem)

    @pl.when(g == 0)
    def _():
        wcopy.start()

    lead, trail = blk_ref[0], blk_ref[1]
    tile = 4 * BLK
    lanes = tot_s.shape[-1]
    per = tile // BLK
    front = seq // 2 // tile
    num_trail = lax.div(trail + 1 + per - 1, per) - front
    num_lead = lax.div(lead + 1 + per - 1, per)
    factor = LOG2_E * BLK ** -0.5
    acc_s[...] = jnp.zeros_like(acc_s)
    tot_s[...] = jnp.zeros_like(tot_s)
    top_s[...] = jnp.full_like(top_s, NEG_BIG)

    def update(chains):
        scores = []
        for slot, qrow, t, limit in chains:
            rows = pl.ds(pl.multiple_of(t * tile, tile), tile)
            for h in range(2):
                q = q_ref[pl.ds(qrow, BLK), h * BLK:(h + 1) * BLK]
                s = lax.dot_general(q, k_ref[rows, :], (((1,), (1,)), ((), ())), preferred_element_type=jnp.float32)
                if limit is not None:
                    ahead = lax.broadcasted_iota(jnp.int32, s.shape, 1) - lax.broadcasted_iota(jnp.int32, s.shape, 0)
                    s = jnp.where(ahead <= limit, s, NEG_BIG)
                scores.append((s, slot, h, rows))
        for s, slot, h, rows in scores:
            top = top_s[slot, h]
            new = jnp.maximum(top, jnp.max(s, axis=-1, keepdims=True))
            fix = jnp.exp2((top - new) * factor)
            e = jnp.exp2((s - new) * factor)
            part = functools.reduce(jnp.add, [e[:, i * lanes:(i + 1) * lanes] for i in range(tile // lanes)])
            tot_s[slot, h] = tot_s[slot, h] * fix + part
            acc_s[slot, h] = acc_s[slot, h] * fix + jnp.dot(e.astype(jnp.bfloat16), v_ref[rows, :], preferred_element_type=jnp.float32)
            top_s[slot, h] = new

    def second(j):
        late = j < num_trail
        t = jnp.where(late, front + j, j - num_trail)
        limit = jnp.where(late, trail, lead) * BLK - t * tile
        return jnp.where(late, 1, 2), pl.multiple_of(jnp.where(late, BLK, 0), BLK), t, limit

    @pl.loop(0, front)
    def _(j):
        update([(0, BLK, j, None), second(j)])

    @pl.loop(front, num_trail + num_lead)
    def _(j):
        update([second(j)])

    for h in range(2):
        cols = pl.ds(pl.multiple_of(g * 2 * BLK + h * BLK, BLK), BLK)
        new = jnp.maximum(top_s[0, h], top_s[1, h])
        fixes = [jnp.exp2((top_s[i, h] - new) * factor) for i in range(2)]
        total = jnp.sum(tot_s[0, h] * fixes[0] + tot_s[1, h] * fixes[1], axis=-1, keepdims=True)
        o_s[BLK:, cols] = ((acc_s[0, h] * fixes[0] + acc_s[1, h] * fixes[1]) / total).astype(jnp.bfloat16)
        o_s[:BLK, cols] = (acc_s[2, h] / jnp.sum(tot_s[2, h], axis=-1, keepdims=True)).astype(jnp.bfloat16)

    @pl.when(g == pl.num_programs(0) - 1)
    def _():
        wcopy.wait()
        output_rows(o_s, w_s, x_ref, out_ref, upd_s)


def causal_layer(blocks, q, k_all, v_all, x, w_out, layer):
    rows, dim = x.shape
    seq = k_all.shape[0]
    kv = pl.BlockSpec((seq, BLK), lambda g, b: (0, g))
    row = pl.BlockSpec((rows, dim), lambda g, b: (0, 0))
    return pl.pallas_call(
        functools.partial(causal_kernel, layer, seq),
        grid_spec=pltpu.PrefetchScalarGridSpec(
            num_scalar_prefetch=1,
            grid=(k_all.shape[1] // BLK,),
            in_specs=[pl.BlockSpec((rows, 2 * BLK), lambda g, b: (0, g)), kv, kv, row, pl.BlockSpec(memory_space=pl.ANY)],
            out_specs=row,
            scratch_shapes=[
                pltpu.VMEM(q.shape, jnp.bfloat16),
                pltpu.VMEM(w_out.shape[1:], jnp.bfloat16),
                pltpu.VMEM((rows, dim), jnp.float32),
                pltpu.VMEM((3, 2, BLK, BLK), jnp.float32),
                pltpu.VMEM((3, 2, BLK, 1), jnp.float32),
                pltpu.VMEM((3, 2, BLK, 128), jnp.float32),
                pltpu.SemaphoreType.DMA,
            ],
        ),
        out_shape=jax.ShapeDtypeStruct((rows, dim), jnp.bfloat16),
        compiler_params=params(),
        cost_estimate=pl.CostEstimate(flops=30 * 10 ** 9, bytes_accessed=2 * w_out[0].size, transcendentals=0),
        name="causal",
    )(blocks, q, k_all, v_all, x, w_out)


def solution(mesh):
    num_dev = mesh.shape["cp"]

    def ring(hop):
        return [(i, (i + hop) % num_dev) for i in range(num_dev)]

    def per_device(hidden, w_query, w_key, w_value, w_out):
        rank = lax.axis_index("cp")
        num_layers = w_query.shape[0]
        rows, dim = hidden.shape
        w_out = w_out.reshape(num_layers, -1, dim)
        last = num_layers - 1
        x = hidden
        for layer in range(last):
            chunk = lax.rem(rank + layer + 1, num_dev).astype(jnp.int32).reshape(1)
            x_next = lax.ppermute(x, "cp", ring(-1))
            k_own, v_own = project(x, (w_key, w_value), layer)
            k_halo = lax.ppermute(k_own, "cp", ring(1))
            v_halo = lax.ppermute(v_own, "cp", ring(1))
            q, k_cur, v_cur = project(x_next, (w_query, w_key, w_value), layer)
            x = window_layer(chunk, q, (k_halo, v_halo, k_own, v_own, k_cur, v_cur), x_next, w_out, layer)

        k_all, v_all, x_all = gather_keys(x, w_key, w_value, last, last, num_dev)
        half = rows // 2
        blocks = jnp.stack([rank, 2 * num_dev - 1 - rank]).astype(jnp.int32)
        rows_fin = []
        for i in range(2):
            owner = lax.rem(blocks[i] // 2 - last + num_dev, num_dev)
            rows_fin.append(lax.dynamic_slice(x_all, (owner, lax.rem(blocks[i], 2) * half, jnp.int32(0)), (1, half, dim)).reshape(half, dim))
        x_fin = jnp.concatenate(rows_fin, axis=0)
        q, = project(x_fin, (w_query,), last)
        return causal_layer(blocks, q, k_all.reshape(-1, k_all.shape[-1]), v_all.reshape(-1, v_all.shape[-1]), x_fin, w_out, last)

    row_spec = P(("dp", "cp"), None)
    return jax.shard_map(per_device, mesh=mesh, in_specs=(row_spec, P(), P(), P(), P()), out_specs=row_spec, check_vma=False)
```

time: 1190 us -> 672 us (0.56)
  Pallas kernels: 0 us -> 582 us
  waiting for transfers between devices: 496 us -> 56.3 us
  matrix products: 429 us -> 0 us
  local copies, waits for them, and re-layouts: 120 us -> 6.52 us
  other arithmetic: 62.9 us -> 2.21 us
  starting transfers between devices: 52 us -> 16.1 us
  between operations: 15 us -> 0.62 us
    pallas_call x0 -> x18, Pallas kernels: none -> 582 us  [the longest x1 215 us: gather_keys(): pl.pallas_call(functools.partial(gather_kernel, num_dev, layer, shift), i...]
    dot_general x110 -> x0, matrix products: 429 us -> none  [the longest x33 133 us: kv_step(): jnp.einsum('hgqk,khd->hgqd', weights.astype(jnp.bfloat16), kv_block[1], p...]
    ppermute x12 -> x15, waiting for transfers between devices: 314 us -> 56.3 us  [the longest x5 56.3 us: per_device(): x_next = lax.ppermute(x, 'cp', ring(-1))]
    all_gather x1 -> x0, waiting for transfers between devices: 182 us -> none  [global_layer(): kv_all = lax.all_gather(jnp.stack([key_rows, value_rows]), 'cp')]
    slice x10 -> x0, local copies, waits for them, and re-layouts: 80 us -> none  [the longest x1 38.4 us: per_device(): w_query[last_layer]]
    reduce_sum x49 -> x0, other arithmetic: 46 us -> none  [the longest x10 21.5 us: window_attention(): row_sum = jnp.sum(weights, axis=-1)]
    ppermute x12 -> x15, starting transfers between devices: 52 us -> 16.1 us  [the longest x5 15.2 us: per_device(): x_next = lax.ppermute(x, 'cp', ring(-1))]
    unnamed x116 -> x10, local copies, waits for them, and re-layouts: 26.8 us -> 4.73 us
  transfers between devices with their start and end apart: 13 -> 15, of which waited for: 12 -> 5; matrix products, arithmetic and copies ran while one was open for 7% -> 0% of each run, Pallas kernels for 0% -> 29%
where the time goes in v1:
time: 672 us; the launch traced here: 663 us
  Pallas kernels  582 us (87%)
  waiting for transfers between devices  56.3 us (8%)
  starting transfers between devices  16.1 us (2%)
    pallas_call x1, Pallas kernels, gather_keys(): pl.pallas_call(functools.partial(gather_kernel, num_dev, layer, shift), i...  215 us
    pallas_call x11, Pallas kernels, project(): pl.pallas_call(functools.partial(proj_kernel, layer, num_w, num_parts), i...  206 us
    pallas_call x5, Pallas kernels, window_layer(): pl.pallas_call(functools.partial(window_kernel, layer), grid_spec=pltpu.P...  106 us
    ppermute x5, waiting for transfers between devices, per_device(): x_next = lax.ppermute(x, 'cp', ring(-1))  56.3 us
    pallas_call x1, Pallas kernels, causal_layer(): pl.pallas_call(functools.partial(causal_kernel, layer, seq), grid_spec=pl...  54.9 us
    ppermute x5, starting transfers between devices, per_device(): x_next = lax.ppermute(x, 'cp', ring(-1))  15.2 us
  transfers between devices with their start and end apart: 15, of which 5 were waited for; matrix products, arithmetic and copies ran while one was open for 0% of the time, Pallas kernels for 29%

profile of v1, /device:TPU:21, one launch (start us, length us, event | category | flops | bytes accessed | tf_op | source)
XLA Modules:
  0.0 663.4 jit_solution(15605613987406313331)
XLA Ops:
  0.0 4.7 collective-permute-start
  4.7 14.0 %proj2.5 = (bf16[512,1024]{1,0:T(8,128)(2,1)}, bf16[512,1024]{1,0:T(8,128)(2,1)}) custom-call(bf16[512,2304]{1,0:T(8,128)(2,1)} %refs_0_.1, bf16[6,2304,4,256]{3,2,1,0:T(4,128)(2,1)} %wk_hbm.1, bf16[6,2304,4,256]{3,2,1,0:T(4,128)(2,1)} %wv_hbm.1), custom_call_target="tpu_custom_call" | custom-call | flops 4831838208 | bytes 9437184 | tf_op jit(solution)/shard_map/proj2/pallas_call | solution.py:78
  18.7 0.1 collective-permute-start.1
  18.8 0.1 collective-permute-start.2
  18.9 11.1 %collective-permute-done.refs_0_.refs_6_ = bf16[512,2304]{1,0:T(8,128)(2,1)} collective-permute-done((bf16[512,2304]{1,0:T(8,128)(2,1)}, bf16[512,2304]{1,0:T(8,128)(2,1)}, u32[]{:S(2)}, u32[]{:S(2)}) %collective-permute-start) | collective-permute-done | bytes 2359328 | tf_op jit(solution)/shard_map/ppermute | solution.py:457
  30.0 24.2 %proj3.5 = (bf16[512,2048]{1,0:T(8,128)(2,1)}, bf16[512,1024]{1,0:T(8,128)(2,1)}, bf16[512,1024]{1,0:T(8,128)(2,1)}) custom-call(bf16[512,2304]{1,0:T(8,128)(2,1)} %collective-permute-done.refs_0_.refs_6_, bf16[6,2304,8,256]{3,2,1,0:T(8,128)(2,1)} %refs_1_.21, bf16[6,2304,4,256]{3,2,1,0:T(4,128)(2,1)} %wk_hbm.1, bf16[6,2304,4,256]{3,2,1,0:T(4,128)(2,1)} %wv_hbm.1), custom_call_target="tpu_custom_call" | custom-call | flops 9663676416 | bytes 18874368 | tf_op jit(solution)/shard_map/proj3/pallas_call | solution.py:78
  54.2 0.0 collective-permute-done.1.refs_0_
  54.2 0.0 copy-start.1
  54.2 0.0 collective-permute-done.2.refs_1_
  54.2 0.9 copy-done.1
  55.2 21.3 %window.5.refs_0_ = bf16[512,2304]{1,0:T(8,128)(2,1)} custom-call(s32[1]{0:T(128)} %bitcast.6.c_ref, bf16[512,2048]{1,0:T(8,128)(2,1)} %get-tuple-element.33.q_ref, bf16[512,1024]{1,0:T(8,128)(2,1)} %copy-done.1, bf16[512,1024]{1,0:T(8,128)(2,1)} %collective-permute-done.2.refs_1_, bf16[512,1024]{1,0:T(8,128)(2,1)} %get-tuple-element.34.refs_2_, ...), custom_call_target="tpu_custom_call" | custom-call | flops 15000000512 | bytes 9437184 | tf_op jit(solution)/shard_map/window/pallas_call | solution.py:166
  76.4 3.1 collective-permute-start.3
  79.6 14.3 %proj2.6 = (bf16[512,1024]{1,0:T(8,128)(2,1)}, bf16[512,1024]{1,0:T(8,128)(2,1)}) custom-call(bf16[512,2304]{1,0:T(8,128)(2,1)} %window.5.refs_0_, bf16[6,2304,4,256]{3,2,1,0:T(4,128)(2,1)} %wk_hbm.1, bf16[6,2304,4,256]{3,2,1,0:T(4,128)(2,1)} %wv_hbm.1), custom_call_target="tpu_custom_call" | custom-call | flops 4831838208 | bytes 9437184 | tf_op jit(solution)/shard_map/proj2/pallas_call | solution.py:78
  93.8 0.1 collective-permute-start.4
  93.9 0.1 collective-permute-start.5
  94.0 11.1 %collective-permute-done.3.refs_0_.refs_6_ = bf16[512,2304]{1,0:T(8,128)(2,1)} collective-permute-done((bf16[512,2304]{1,0:T(8,128)(2,1)}, bf16[512,2304]{1,0:T(8,128)(2,1)}, u32[]{:S(2)}, u32[]{:S(2)}) %collective-permute-start.3) | collective-permute-done | bytes 2359328 | tf_op jit(solution)/shard_map/ppermute | solution.py:457
  105.1 24.2 %proj3.6 = (bf16[512,2048]{1,0:T(8,128)(2,1)}, bf16[512,1024]{1,0:T(8,128)(2,1)}, bf16[512,1024]{1,0:T(8,128)(2,1)}) custom-call(bf16[512,2304]{1,0:T(8,128)(2,1)} %collective-permute-done.3.refs_0_.refs_6_, bf16[6,2304,8,256]{3,2,1,0:T(8,128)(2,1)} %refs_1_.21, bf16[6,2304,4,256]{3,2,1,0:T(4,128)(2,1)} %wk_hbm.1, bf16[6,2304,4,256]{3,2,1,0:T(4,128)(2,1)} %wv_hbm.1), custom_call_target="tpu_custom_call" | custom-call | flops 9663676416 | bytes 18874368 | tf_op jit(solution)/shard_map/proj3/pallas_call | solution.py:78
  129.3 0.0 collective-permute-done.4.refs_0_
  129.3 0.0 copy-start.2
  129.3 0.0 collective-permute-done.5.refs_1_
  129.3 0.9 copy-done.2
  130.2 21.0 %window.6.refs_0_ = bf16[512,2304]{1,0:T(8,128)(2,1)} custom-call(s32[1]{0:T(128)} %bitcast.5.c_ref, bf16[512,2048]{1,0:T(8,128)(2,1)} %get-tuple-element.38.q_ref, bf16[512,1024]{1,0:T(8,128)(2,1)} %copy-done.2, bf16[512,1024]{1,0:T(8,128)(2,1)} %collective-permute-done.5.refs_1_, bf16[512,1024]{1,0:T(8,128)(2,1)} %get-tuple-element.39.refs_2_, ...), custom_call_target="tpu_custom_call" | custom-call | flops 15000000512 | bytes 9437184 | tf_op jit(solution)/shard_map/window/pallas_call | solution.py:166
  151.3 2.6 collective-permute-start.6
  153.8 14.3 %proj2.7 = (bf16[512,1024]{1,0:T(8,128)(2,1)}, bf16[512,1024]{1,0:T(8,128)(2,1)}) custom-call(bf16[512,2304]{1,0:T(8,128)(2,1)} %window.6.refs_0_, bf16[6,2304,4,256]{3,2,1,0:T(4,128)(2,1)} %wk_hbm.1, bf16[6,2304,4,256]{3,2,1,0:T(4,128)(2,1)} %wv_hbm.1), custom_call_target="tpu_custom_call" | custom-call | flops 4831838208 | bytes 9437184 | tf_op jit(solution)/shard_map/proj2/pallas_call | solution.py:78
  168.2 0.1 collective-permute-start.7
  168.3 0.1 collective-permute-start.8
  168.3 11.5 %collective-permute-done.6.refs_0_.refs_6_ = bf16[512,2304]{1,0:T(8,128)(2,1)} collective-permute-done((bf16[512,2304]{1,0:T(8,128)(2,1)}, bf16[512,2304]{1,0:T(8,128)(2,1)}, u32[]{:S(2)}, u32[]{:S(2)}) %collective-permute-start.6) | collective-permute-done | bytes 2359328 | tf_op jit(solution)/shard_map/ppermute | solution.py:457
  179.9 24.2 %proj3.7 = (bf16[512,2048]{1,0:T(8,128)(2,1)}, bf16[512,1024]{1,0:T(8,128)(2,1)}, bf16[512,1024]{1,0:T(8,128)(2,1)}) custom-call(bf16[512,2304]{1,0:T(8,128)(2,1)} %collective-permute-done.6.refs_0_.refs_6_, bf16[6,2304,8,256]{3,2,1,0:T(8,128)(2,1)} %refs_1_.21, bf16[6,2304,4,256]{3,2,1,0:T(4,128)(2,1)} %wk_hbm.1, bf16[6,2304,4,256]{3,2,1,0:T(4,128)(2,1)} %wv_hbm.1), custom_call_target="tpu_custom_call" | custom-call | flops 9663676416 | bytes 18874368 | tf_op jit(solution)/shard_map/proj3/pallas_call | solution.py:78
  204.1 0.0 collective-permute-done.7.refs_0_
  204.1 0.0 copy-start.3
  204.1 0.0 collective-permute-done.8.refs_1_
  204.1 0.9 copy-done.3
  205.1 21.3 %window.7.refs_0_ = bf16[512,2304]{1,0:T(8,128)(2,1)} custom-call(s32[1]{0:T(128)} %bitcast.4.c_ref, bf16[512,2048]{1,0:T(8,128)(2,1)} %get-tuple-element.43.q_ref, bf16[512,1024]{1,0:T(8,128)(2,1)} %copy-done.3, bf16[512,1024]{1,0:T(8,128)(2,1)} %collective-permute-done.8.refs_1_, bf16[512,1024]{1,0:T(8,128)(2,1)} %get-tuple-element.44.refs_2_, ...), custom_call_target="tpu_custom_call" | custom-call | flops 15000000512 | bytes 9437184 | tf_op jit(solution)/shard_map/window/pallas_call | solution.py:166
  226.4 2.0 collective-permute-start.9
  228.3 14.3 %proj2.8 = (bf16[512,1024]{1,0:T(8,128)(2,1)}, bf16[512,1024]{1,0:T(8,128)(2,1)}) custom-call(bf16[512,2304]{1,0:T(8,128)(2,1)} %window.7.refs_0_, bf16[6,2304,4,256]{3,2,1,0:T(4,128)(2,1)} %wk_hbm.1, bf16[6,2304,4,256]{3,2,1,0:T(4,128)(2,1)} %wv_hbm.1), custom_call_target="tpu_custom_call" | custom-call | flops 4831838208 | bytes 9437184 | tf_op jit(solution)/shard_map/proj2/pallas_call | solution.py:78
  242.6 0.1 collective-permute-start.10
  242.7 0.3 collective-permute-start.11
  243.0 12.0 %collective-permute-done.9.refs_0_.refs_6_ = bf16[512,2304]{1,0:T(8,128)(2,1)} collective-permute-done((bf16[512,2304]{1,0:T(8,128)(2,1)}, bf16[512,2304]{1,0:T(8,128)(2,1)}, u32[]{:S(2)}, u32[]{:S(2)}) %collective-permute-start.9) | collective-permute-done | bytes 2359328 | tf_op jit(solution)/shard_map/ppermute | solution.py:457
  255.0 24.3 %proj3.8 = (bf16[512,2048]{1,0:T(8,128)(2,1)}, bf16[512,1024]{1,0:T(8,128)(2,1)}, bf16[512,1024]{1,0:T(8,128)(2,1)}) custom-call(bf16[512,2304]{1,0:T(8,128)(2,1)} %collective-permute-done.9.refs_0_.refs_6_, bf16[6,2304,8,256]{3,2,1,0:T(8,128)(2,1)} %refs_1_.21, bf16[6,2304,4,256]{3,2,1,0:T(4,128)(2,1)} %wk_hbm.1, bf16[6,2304,4,256]{3,2,1,0:T(4,128)(2,1)} %wv_hbm.1), custom_call_target="tpu_custom_call" | custom-call | flops 9663676416 | bytes 18874368 | tf_op jit(solution)/shard_map/proj3/pallas_call | solution.py:78
  279.2 0.0 collective-permute-done.10.refs_0_
  279.3 0.0 copy-start.4
  279.3 0.0 collective-permute-done.11.refs_1_
  279.3 0.9 copy-done.4
  280.2 21.0 %window.8.refs_0_ = bf16[512,2304]{1,0:T(8,128)(2,1)} custom-call(s32[1]{0:T(128)} %bitcast.3.c_ref, bf16[512,2048]{1,0:T(8,128)(2,1)} %get-tuple-element.48.q_ref, bf16[512,1024]{1,0:T(8,128)(2,1)} %copy-done.4, bf16[512,1024]{1,0:T(8,128)(2,1)} %collective-permute-done.11.refs_1_, bf16[512,1024]{1,0:T(8,128)(2,1)} %get-tuple-element.49.refs_2_, ...), custom_call_target="tpu_custom_call" | custom-call | flops 15000000512 | bytes 9437184 | tf_op jit(solution)/shard_map/window/pallas_call | solution.py:166
  301.2 2.9 collective-permute-start.12
  304.1 14.3 %proj2.9 = (bf16[512,1024]{1,0:T(8,128)(2,1)}, bf16[512,1024]{1,0:T(8,128)(2,1)}) custom-call(bf16[512,2304]{1,0:T(8,128)(2,1)} %window.8.refs_0_, bf16[6,2304,4,256]{3,2,1,0:T(4,128)(2,1)} %wk_hbm.1, bf16[6,2304,4,256]{3,2,1,0:T(4,128)(2,1)} %wv_hbm.1), custom_call_target="tpu_custom_call" | custom-call | flops 4831838208 | bytes 9437184 | tf_op jit(solution)/shard_map/proj2/pallas_call | solution.py:78
  318.4 0.1 collective-permute-start.13
  318.5 0.1 collective-permute-start.14
  318.6 0.6 pad_add_fusion.blk_ref
  319.2 10.6 %collective-permute-done.12.refs_0_.refs_6_ = bf16[512,2304]{1,0:T(8,128)(2,1)} collective-permute-done((bf16[512,2304]{1,0:T(8,128)(2,1)}, bf16[512,2304]{1,0:T(8,128)(2,1)}, u32[]{:S(2)}, u32[]{:S(2)}) %collective-permute-start.12) | collective-permute-done | bytes 2359328 | tf_op jit(solution)/shard_map/ppermute | solution.py:457
  329.9 24.3 %proj3.9 = (bf16[512,2048]{1,0:T(8,128)(2,1)}, bf16[512,1024]{1,0:T(8,128)(2,1)}, bf16[512,1024]{1,0:T(8,128)(2,1)}) custom-call(bf16[512,2304]{1,0:T(8,128)(2,1)} %collective-permute-done.12.refs_0_.refs_6_, bf16[6,2304,8,256]{3,2,1,0:T(8,128)(2,1)} %refs_1_.21, bf16[6,2304,4,256]{3,2,1,0:T(4,128)(2,1)} %wk_hbm.1, bf16[6,2304,4,256]{3,2,1,0:T(4,128)(2,1)} %wv_hbm.1), custom_call_target="tpu_custom_call" | custom-call | flops 9663676416 | bytes 18874368 | tf_op jit(solution)/shard_map/proj3/pallas_call | solution.py:78
  354.2 0.0 collective-permute-done.13.refs_0_
  354.2 0.0 copy-start
  354.2 0.0 collective-permute-done.14.refs_1_
  354.2 0.9 copy-done
  355.2 21.3 %window.9.x_hbm = bf16[512,2304]{1,0:T(8,128)(2,1)} custom-call(s32[1]{0:T(128)} %bitcast.2.c_ref, bf16[512,2048]{1,0:T(8,128)(2,1)} %get-tuple-element.53.q_ref, bf16[512,1024]{1,0:T(8,128)(2,1)} %copy-done, bf16[512,1024]{1,0:T(8,128)(2,1)} %collective-permute-done.14.refs_1_, bf16[512,1024]{1,0:T(8,128)(2,1)} %get-tuple-element.54.refs_2_, ...), custom_call_target="tpu_custom_call" | custom-call | flops 15000000512 | bytes 9437184 | tf_op jit(solution)/shard_map/window/pallas_call | solution.py:166
  376.5 215.3 %gather.1 = (bf16[16,512,1024]{2,1,0:T(8,128)(2,1)}, bf16[16,512,1024]{2,1,0:T(8,128)(2,1)}, bf16[16,512,2304]{2,1,0:T(8,128)(2,1)}) custom-call(bf16[512,2304]{1,0:T(8,128)(2,1)} %window.9.x_hbm, bf16[6,2304,4,256]{3,2,1,0:T(4,128)(2,1)} %wk_hbm.1, bf16[6,2304,4,256]{3,2,1,0:T(4,128)(2,1)} %wv_hbm.1), custom_call_target="tpu_custom_call" | custom-call | flops 77309411328 | bytes 9437184 | tf_op jit(solution)/shard_map/gather/pallas_call | solution.py:330
  591.8 1.8 dynamic-slice_bitcast_fusion.1
  593.5 1.6 pad_maximum_fusion.refs_0_.x_ref
  595.1 13.1 %proj1.1.q_ref = bf16[512,2048]{1,0:T(8,128)(2,1)} custom-call(bf16[512,2304]{1,0:T(8,128)(2,1)} %pad_maximum_fusion.refs_0_.x_ref, bf16[6,2304,8,256]{3,2,1,0:T(8,128)(2,1)} %refs_1_.21), custom_call_target="tpu_custom_call" | custom-call | flops 4831838208 | bytes 9437184 | tf_op jit(solution)/shard_map/proj1/pallas_call | solution.py:78
  608.3 54.9 %causal.1 = bf16[512,2304]{1,0:T(8,128)(2,1)} custom-call(s32[2]{0:T(128)} %pad_add_fusion.blk_ref, bf16[512,2048]{1,0:T(8,128)(2,1)} %proj1.1.q_ref, bf16[8192,1024]{1,0:T(8,128)(2,1)} %bitcast.20, bf16[8192,1024]{1,0:T(8,128)(2,1)} %bitcast.21, bf16[512,2304]{1,0:T(8,128)(2,1)} %pad_maximum_fusion.refs_0_.x_ref, bf16[6,2048,2304]{2,1,0:T(8,128)(2,1)} %bitcast.19), custom_call_target="tpu_custom_call" | custom-call | flops 30000001024 | bytes 9437184 | tf_op jit(solution)/shard_map/causal/pallas_call | solution.py:418
Async XLA Ops:
  0.0 30.0 %collective-permute-start = (bf16[512,2304]{1,0:T(8,128)(2,1)}, bf16[512,2304]{1,0:T(8,128)(2,1)}, u32[]{:S(2)}, u32[]{:S(2)}) collective-permute-start(bf16[512,2304]{1,0:T(8,128)(2,1)} %refs_0_.1), channel_id=1, source_target_pairs={{0,15},{1,0},{2,1},{3,2},{4,3},{5,4},{6,5},{7,6},{8,7},{9,8},{10,9... | collective-permute-start | bytes 7077896 | tf_op jit(solution)/shard_map/ppermute | solution.py:457
  18.7 35.5 %collective-permute-start.1 = (bf16[512,1024]{1,0:T(8,128)(2,1)}, bf16[512,1024]{1,0:T(8,128)(2,1)S(1)}, u32[]{:S(2)}, u32[]{:S(2)}) collective-permute-start(bf16[512,1024]{1,0:T(8,128)(2,1)} %get-tuple-element.34.refs_2_), channel_id=1, source_target_pairs={{0,1},{1,2},{2,3},{3,4},{4,5},{5,6},{6,7},{7,8},{8,9},{9,10},{10,1... | collective-permute-start | bytes 3145736 | tf_op jit(solution)/shard_map/ppermute | solution.py:459
  18.8 35.4 %collective-permute-start.2 = (bf16[512,1024]{1,0:T(8,128)(2,1)}, bf16[512,1024]{1,0:T(8,128)(2,1)}, u32[]{:S(2)}, u32[]{:S(2)}) collective-permute-start(bf16[512,1024]{1,0:T(8,128)(2,1)} %get-tuple-element.35.refs_3_), channel_id=1, source_target_pairs={{0,1},{1,2},{2,3},{3,4},{4,5},{5,6},{6,7},{7,8},{8,9},{9,10},{10,1... | collective-permute-start | bytes 3145736 | tf_op jit(solution)/shard_map/ppermute | solution.py:460
  54.2 1.0 copy-start.1
  76.4 28.6 %collective-permute-start.3 = (bf16[512,2304]{1,0:T(8,128)(2,1)}, bf16[512,2304]{1,0:T(8,128)(2,1)}, u32[]{:S(2)}, u32[]{:S(2)}) collective-permute-start(bf16[512,2304]{1,0:T(8,128)(2,1)} %window.5.refs_0_), channel_id=1, source_target_pairs={{0,15},{1,0},{2,1},{3,2},{4,3},{5,4},{6,5},{7,6},{8,7},{9,8},{10,9... | collective-permute-start | bytes 7077896 | tf_op jit(solution)/shard_map/ppermute | solution.py:457
  93.8 35.4 %collective-permute-start.4 = (bf16[512,1024]{1,0:T(8,128)(2,1)}, bf16[512,1024]{1,0:T(8,128)(2,1)S(1)}, u32[]{:S(2)}, u32[]{:S(2)}) collective-permute-start(bf16[512,1024]{1,0:T(8,128)(2,1)} %get-tuple-element.39.refs_2_), channel_id=1, source_target_pairs={{0,1},{1,2},{2,3},{3,4},{4,5},{5,6},{6,7},{7,8},{8,9},{9,10},{10,1... | collective-permute-start | bytes 3145736 | tf_op jit(solution)/shard_map/ppermute | solution.py:459
  93.9 35.4 %collective-permute-start.5 = (bf16[512,1024]{1,0:T(8,128)(2,1)}, bf16[512,1024]{1,0:T(8,128)(2,1)}, u32[]{:S(2)}, u32[]{:S(2)}) collective-permute-start(bf16[512,1024]{1,0:T(8,128)(2,1)} %get-tuple-element.40.refs_3_), channel_id=1, source_target_pairs={{0,1},{1,2},{2,3},{3,4},{4,5},{5,6},{6,7},{7,8},{8,9},{9,10},{10,1... | collective-permute-start | bytes 3145736 | tf_op jit(solution)/shard_map/ppermute | solution.py:460
  129.3 1.0 copy-start.2
  151.3 28.6 %collective-permute-start.6 = (bf16[512,2304]{1,0:T(8,128)(2,1)}, bf16[512,2304]{1,0:T(8,128)(2,1)}, u32[]{:S(2)}, u32[]{:S(2)}) collective-permute-start(bf16[512,2304]{1,0:T(8,128)(2,1)} %window.6.refs_0_), channel_id=1, source_target_pairs={{0,15},{1,0},{2,1},{3,2},{4,3},{5,4},{6,5},{7,6},{8,7},{9,8},{10,9... | collective-permute-start | bytes 7077896 | tf_op jit(solution)/shard_map/ppermute | solution.py:457
  168.2 35.9 %collective-permute-start.7 = (bf16[512,1024]{1,0:T(8,128)(2,1)}, bf16[512,1024]{1,0:T(8,128)(2,1)S(1)}, u32[]{:S(2)}, u32[]{:S(2)}) collective-permute-start(bf16[512,1024]{1,0:T(8,128)(2,1)} %get-tuple-element.44.refs_2_), channel_id=1, source_target_pairs={{0,1},{1,2},{2,3},{3,4},{4,5},{5,6},{6,7},{7,8},{8,9},{9,10},{10,1... | collective-permute-start | bytes 3145736 | tf_op jit(solution)/shard_map/ppermute | solution.py:459
  168.3 35.9 %collective-permute-start.8 = (bf16[512,1024]{1,0:T(8,128)(2,1)}, bf16[512,1024]{1,0:T(8,128)(2,1)}, u32[]{:S(2)}, u32[]{:S(2)}) collective-permute-start(bf16[512,1024]{1,0:T(8,128)(2,1)} %get-tuple-element.45.refs_3_), channel_id=1, source_target_pairs={{0,1},{1,2},{2,3},{3,4},{4,5},{5,6},{6,7},{7,8},{8,9},{9,10},{10,1... | collective-permute-start | bytes 3145736 | tf_op jit(solution)/shard_map/ppermute | solution.py:460
  204.1 1.0 copy-start.3
  226.4 28.6 %collective-permute-start.9 = (bf16[512,2304]{1,0:T(8,128)(2,1)}, bf16[512,2304]{1,0:T(8,128)(2,1)}, u32[]{:S(2)}, u32[]{:S(2)}) collective-permute-start(bf16[512,2304]{1,0:T(8,128)(2,1)} %window.7.refs_0_), channel_id=1, source_target_pairs={{0,15},{1,0},{2,1},{3,2},{4,3},{5,4},{6,5},{7,6},{8,7},{9,8},{10,9... | collective-permute-start | bytes 7077896 | tf_op jit(solution)/shard_map/ppermute | solution.py:457
  242.6 36.7 %collective-permute-start.10 = (bf16[512,1024]{1,0:T(8,128)(2,1)}, bf16[512,1024]{1,0:T(8,128)(2,1)S(1)}, u32[]{:S(2)}, u32[]{:S(2)}) collective-permute-start(bf16[512,1024]{1,0:T(8,128)(2,1)} %get-tuple-element.49.refs_2_), channel_id=1, source_target_pairs={{0,1},{1,2},{2,3},{3,4},{4,5},{5,6},{6,7},{7,8},{8,9},{9,10},{10,1... | collective-permute-start | bytes 3145736 | tf_op jit(solution)/shard_map/ppermute | solution.py:459
  242.7 36.6 %collective-permute-start.11 = (bf16[512,1024]{1,0:T(8,128)(2,1)}, bf16[512,1024]{1,0:T(8,128)(2,1)}, u32[]{:S(2)}, u32[]{:S(2)}) collective-permute-start(bf16[512,1024]{1,0:T(8,128)(2,1)} %get-tuple-element.50.refs_3_), channel_id=1, source_target_pairs={{0,1},{1,2},{2,3},{3,4},{4,5},{5,6},{6,7},{7,8},{8,9},{9,10},{10,1... | collective-permute-start | bytes 3145736 | tf_op jit(solution)/shard_map/ppermute | solution.py:460
  279.3 1.0 copy-start.4
  301.2 28.6 %collective-permute-start.12 = (bf16[512,2304]{1,0:T(8,128)(2,1)}, bf16[512,2304]{1,0:T(8,128)(2,1)}, u32[]{:S(2)}, u32[]{:S(2)}) collective-permute-start(bf16[512,2304]{1,0:T(8,128)(2,1)} %window.8.refs_0_), channel_id=1, source_target_pairs={{0,15},{1,0},{2,1},{3,2},{4,3},{5,4},{6,5},{7,6},{8,7},{9,8},{10,9... | collective-permute-start | bytes 7077896 | tf_op jit(solution)/shard_map/ppermute | solution.py:457
  318.4 35.8 %collective-permute-start.13 = (bf16[512,1024]{1,0:T(8,128)(2,1)}, bf16[512,1024]{1,0:T(8,128)(2,1)S(1)}, u32[]{:S(2)}, u32[]{:S(2)}) collective-permute-start(bf16[512,1024]{1,0:T(8,128)(2,1)} %get-tuple-element.54.refs_2_), channel_id=1, source_target_pairs={{0,1},{1,2},{2,3},{3,4},{4,5},{5,6},{6,7},{7,8},{8,9},{9,10},{10,1... | collective-permute-start | bytes 3145736 | tf_op jit(solution)/shard_map/ppermute | solution.py:459
  318.5 35.8 %collective-permute-start.14 = (bf16[512,1024]{1,0:T(8,128)(2,1)}, bf16[512,1024]{1,0:T(8,128)(2,1)}, u32[]{:S(2)}, u32[]{:S(2)}) collective-permute-start(bf16[512,1024]{1,0:T(8,128)(2,1)} %get-tuple-element.55.refs_3_), channel_id=1, source_target_pairs={{0,1},{1,2},{2,3},{3,4},{4,5},{5,6},{6,7},{7,8},{8,9},{9,10},{10,1... | collective-permute-start | bytes 3145736 | tf_op jit(solution)/shard_map/ppermute | solution.py:460
  354.2 1.0 copy-start

commit v2 on v1

v2 whole, which is shorter than its diff:
```python
import functools

import jax
import jax.numpy as jnp
from jax import lax
from jax.experimental import pallas as pl
from jax.experimental.pallas import tpu as pltpu
from jax.sharding import PartitionSpec as P

WINDOW = 1024
EPS_NORM = 1e-6
NEG_BIG = -1e30
LOG2_E = 1.4426950408889634
BLK = 256
VMEM_BYTES = 62 << 20
MESH = pl.DeviceIdType.MESH


def params(**kw):
    return pltpu.CompilerParams(vmem_limit_bytes=VMEM_BYTES, **kw)


def normed(rows):
    wide = rows.astype(jnp.float32)
    return (wide * lax.rsqrt(jnp.mean(wide * wide, axis=-1, keepdims=True) + EPS_NORM)).astype(jnp.bfloat16)


def output_rows(o_s, w_s, x_ref, out_ref, upd_s):
    rows, dim = x_ref.shape
    tile = 768

    @pl.loop(0, dim // tile)
    def _(s):
        cols = pl.ds(pl.multiple_of(s * tile, tile), tile)
        upd_s[:, cols] = jnp.dot(o_s[...], w_s[:, cols], preferred_element_type=jnp.float32)

    @pl.loop(0, rows // 64)
    def _(s):
        part = pl.ds(pl.multiple_of(s * 64, 64), 64)
        upd = upd_s[part, :]
        scale = lax.rsqrt(jnp.mean(upd * upd, axis=-1, keepdims=True) + EPS_NORM)
        out_ref[part, :] = (x_ref[part, :].astype(jnp.float32) + upd * scale).astype(jnp.bfloat16)


def scoped(name):
    def wrap(fn):
        def run(*args):
            with jax.named_scope(name):
                return fn(*args)

        return run

    return wrap


def stack_kernel(num_dev, num_layers, x_hbm, wq_hbm, wk_hbm, wv_hbm, wo_hbm, out_hbm,
                 xr, xn, kv, n_s, q_s, wq_s, wkv_s, wo_s, upd_s, stq, stk, stv,
                 x_send, x_recv, h_send, h_recv, c_send, c_recv, h_free, c_free, xsem, qsem, ksem, vsem, wsem):
    blk, dim = n_s.shape
    width = wkv_s.shape[1] // 2
    heads = q_s.shape[2] // width
    head = BLK
    q_rows, kv_rows = stq.shape[1], stk.shape[1]
    q_ring, kv_ring = stq.shape[0], stk.shape[0]
    q_parts, kv_parts = dim // q_rows, dim // kv_rows
    me = lax.axis_index("cp")
    odd = lax.rem(me, 2)
    is_odd, is_even = odd == 1, odd == 0
    left, right = lax.rem(me + num_dev - 1, num_dev), lax.rem(me + 1, num_dev)

    def block(i):
        return pl.ds(pl.multiple_of(i * blk, blk), blk)

    def remote(src, dst, send, recv, dev):
        return pltpu.make_async_remote_copy(src_ref=src, dst_ref=dst, send_sem=send, recv_sem=recv, device_id={"cp": dev}, device_id_type=MESH)

    def x_copy(slot, s):
        return remote(xn.at[s], xr.at[slot, s], x_send.at[s], x_recv.at[slot, s], left)

    def h_copy(s):
        return remote(kv.at[block(2 + s)], kv.at[block(s)], h_send.at[s], h_recv.at[s], right)

    def c_copy(s):
        return remote(kv.at[block(2 + s)], kv.at[block(4 + s)], c_send.at[s], c_recv.at[s], left)

    def signal(sem, dev):
        pl.semaphore_signal(sem, inc=1, device_id={"cp": dev}, device_id_type=MESH)

    def q_stage(layer, i):
        b = lax.rem(layer * q_parts + i, q_ring)
        return pltpu.make_async_copy(wq_hbm.at[layer, pl.ds(i * q_rows, q_rows)], stq.at[b], qsem.at[b])

    def kv_stage(layer, i):
        b = lax.rem(layer * kv_parts + i, kv_ring)
        rows = pl.ds(i * kv_rows, kv_rows)
        return (pltpu.make_async_copy(wk_hbm.at[layer, rows], stk.at[b], ksem.at[b]),
                pltpu.make_async_copy(wv_hbm.at[layer, rows], stv.at[b], vsem.at[b]))

    def kv_start(layer, i):
        for cp in kv_stage(layer, i):
            cp.start()

    def kv_wait(layer, i):
        for cp in kv_stage(layer, i):
            cp.wait()

    def kv_flat(layer, i):
        b = lax.rem(layer * kv_parts + i, kv_ring)
        rows = pl.ds(pl.multiple_of(i * kv_rows, 16), kv_rows)
        wkv_s[rows, :width] = stk[b].reshape(kv_rows, width)
        wkv_s[rows, width:] = stv[b].reshape(kv_rows, width)

    def q_flat(layer, i):
        b = lax.rem(layer * q_parts + i, q_ring)
        wq_s[pl.ds(pl.multiple_of(i * q_rows, 16), q_rows), :] = stq[b].reshape(q_rows, wq_s.shape[1])

    def kv_next(layer, i):
        @pl.when(i + kv_ring < kv_parts)
        def _():
            kv_start(layer, i + kv_ring)

    def q_next(layer, i):
        after = i + q_ring

        @pl.when(after < q_parts)
        def _():
            q_stage(layer, after).start()

        @pl.when((after >= q_parts) & (layer + 1 < num_layers))
        def _():
            q_stage(layer + 1, after - q_parts).start()

    def wo_copy(layer):
        return pltpu.make_async_copy(wo_hbm.at[layer], wo_s, wsem)

    def norm_into(ref):
        step = min(64, blk)

        @pl.loop(0, blk // step)
        def _(i):
            part = pl.ds(pl.multiple_of(i * step, step), step)
            n_s[part, :] = normed(ref[part, :])

    def dot(w):
        return jnp.dot(n_s[...], w, preferred_element_type=jnp.float32).astype(jnp.bfloat16)

    def attend(s, span, start):
        window = WINDOW + blk
        rows = pl.ds(pl.multiple_of(s * blk + window - span, blk), span)
        factor = LOG2_E * head ** -0.5
        groups = width // head
        together = groups if span == window else 2
        qi = lax.broadcasted_iota(jnp.int32, (blk, blk), 0)
        ki = lax.broadcasted_iota(jnp.int32, (blk, blk), 1)

        def scores(item):
            sc = lax.dot_general(q_s[s, :, item[2]], kv[rows, item[0]], (((1,), (1,)), ((), ())), preferred_element_type=jnp.float32)
            last = jnp.where(ki <= qi, sc[:, span - blk:], NEG_BIG)
            if span == window:
                return jnp.concatenate([jnp.where(ki > qi, sc[:, :blk], NEG_BIG), sc[:, blk:span - blk], last], axis=1)
            mid = sc[:, :span - blk]
            pos = lax.broadcasted_iota(jnp.int32, mid.shape, 1)
            return jnp.concatenate([jnp.where(pos >= start - (window - span), mid, NEG_BIG), last], axis=1)

        def finish(sc, item):
            top = jnp.max(sc, axis=-1, keepdims=True)
            e = jnp.exp2((sc - top) * factor)
            total = jnp.sum(e, axis=-1, keepdims=True)
            acc = jnp.dot(e.astype(jnp.bfloat16), kv[rows, item[1]], preferred_element_type=jnp.float32)
            return (acc / total).astype(jnp.bfloat16)

        def some(first):
            items = []
            for u in range(together):
                g = first + u
                for h in range(heads):
                    offsets = (g * head, width + g * head, (g * heads + h) * head)
                    items.append(tuple(pl.ds(o if isinstance(o, int) else pl.multiple_of(o, head), head) for o in offsets))
            ahead = scores(items[0])
            for k, item in enumerate(items):
                now = ahead
                if k + 1 < len(items):
                    ahead = scores(items[k + 1])
                q_s[s, :, item[2]] = finish(now, item)

        if together == groups:
            some(0)
        else:
            @pl.loop(0, groups // together)
            def _(i):
                some(i * together)

    tile = width
    loads = [pltpu.make_async_copy(x_hbm.at[block(s)], xn.at[s], xsem.at[s]) for s in range(2)]
    for cp in loads:
        cp.start()
    for i in range(kv_ring):
        kv_start(0, i)
    for i in range(q_ring):
        q_stage(0, i).start()
    barrier = pltpu.get_barrier_semaphore()
    for dev in (left, right):
        signal(barrier, dev)
    pl.semaphore_wait(barrier, 2)
    for s in range(2):
        loads[s].wait()
        x_copy(0, s).start()

    @pl.loop(0, kv_parts)
    def _(i):
        kv_wait(0, i)
        kv_flat(0, i)
        kv_next(0, i)

    @pl.loop(0, num_layers)
    def _(layer):
        slot = lax.rem(layer, 2)
        more = layer + 1 < num_layers
        chunk = lax.rem(me + layer + 1, num_dev)

        @pl.when(layer > 0)
        def _():
            for s in range(2):
                h_copy(s).wait_send()

            @pl.when(is_odd)
            def _():
                for s in range(2):
                    c_copy(s).wait_send()

        @pl.loop(0, 2)
        def _(s):
            with jax.named_scope("own_norm"):
                norm_into(xn.at[s])

            @pl.loop(0, 2)
            @scoped("own")
            def _(j):
                per = q_parts // 4
                first = (2 * s + j) * per
                for t in range(per):
                    q_stage(layer, first + t).wait()
                    q_flat(layer, first + t)
                    q_next(layer, first + t)
                cols = pl.ds(pl.multiple_of(j * tile, tile), tile)
                kv[block(2 + s), cols] = dot(wkv_s[:, cols])

            @pl.when((layer > 0) & (s == 0))
            @scoped("credit")
            def _():
                pl.semaphore_wait(h_free, 1)

                @pl.when(is_odd)
                def _():
                    pl.semaphore_wait(c_free, 1)

            h_copy(s).start()

            @pl.when(is_odd)
            def _():
                c_copy(s).start()

        wo_copy(layer).start()

        @pl.when(more)
        def _():
            for i in range(kv_ring):
                kv_start(layer + 1, i)

        @pl.loop(0, 2)
        def _(s):
            @pl.loop(jnp.where(is_odd, s, 2 * s), jnp.where(is_odd, s + 1, 2))
            def _(t):
                with jax.named_scope("x_wait"):
                    x_copy(slot, t).wait_recv()
                with jax.named_scope("norm"):
                    norm_into(xr.at[slot, t])

                @pl.loop(0, 2)
                @scoped("query")
                def _(j):
                    cols = pl.ds(pl.multiple_of(j * tile, tile), tile)
                    q_s[t, :, cols] = dot(wq_s[:, cols])

                @pl.when(is_odd)
                def _():
                    @pl.loop(0, 2)
                    @scoped("keys")
                    def _(j):
                        cols = pl.ds(pl.multiple_of(j * tile, tile), tile)
                        kv[block(4 + t), cols] = dot(wkv_s[:, cols])

            @pl.when(s == 0)
            @scoped("h_wait")
            def _():
                for i in range(2):
                    h_copy(i).wait_recv()

            @pl.when(is_even)
            @scoped("c_wait")
            def _():
                c_copy(s).wait_recv()

            for first, cond in ((2, chunk >= 2), (1, chunk == 1), (0, chunk == 0)):
                @pl.when(cond)
                @scoped("attend")
                def _():
                    attend(s, (2 * first + 1) * blk if first == 2 else (2 * first + 2) * blk, WINDOW - s * blk - first * 2 * blk)

            @pl.when((s == 1) & more)
            def _():
                signal(h_free, left)

                @pl.when(is_even)
                def _():
                    signal(c_free, right)

            out_tiles = 3
            out_tile = dim // out_tiles

            @pl.when(s == 0)
            def _():
                wo_copy(layer).wait()

            def out_dot(j):
                cols = pl.ds(pl.multiple_of(j * out_tile, out_tile), out_tile)
                upd_s[:, cols] = jnp.dot(q_s[s], wo_s[:, cols], preferred_element_type=jnp.float32)

            relay = (s == 1) & more

            @pl.when(relay)
            def _():
                @pl.loop(0, out_tiles)
                @scoped("out_lay")
                def _(j):
                    per = kv_parts // out_tiles
                    for t in range(per):
                        kv_wait(layer + 1, j * per + t)
                        kv_flat(layer + 1, j * per + t)
                        kv_next(layer + 1, j * per + t)
                    out_dot(j)

            @pl.when(jnp.logical_not(relay))
            def _():
                @pl.loop(0, out_tiles)
                @scoped("out")
                def _(j):
                    out_dot(j)

            with jax.named_scope("x_sent"):
                x_copy(slot, s).wait_send()
            step = min(64, blk)

            @pl.loop(0, blk // step)
            @scoped("resid")
            def _(i):
                part = pl.ds(pl.multiple_of(i * step, step), step)
                upd = upd_s[part, :]
                scale = lax.rsqrt(jnp.mean(upd * upd, axis=-1, keepdims=True) + EPS_NORM)
                xn[s, part, :] = (xr[slot, s, part, :].astype(jnp.float32) + upd * scale).astype(jnp.bfloat16)

            @pl.when(more)
            def _():
                x_copy(1 - slot, s).start()

            @pl.when(jnp.logical_not(more))
            def _():
                pltpu.make_async_copy(xn.at[s], out_hbm.at[block(s)], xsem.at[s]).start()

    for s in range(2):
        h_copy(s).wait_send()
        pltpu.make_async_copy(xn.at[s], out_hbm.at[block(s)], xsem.at[s]).wait()

    @pl.when(is_odd)
    def _():
        for s in range(2):
            c_copy(s).wait_send()


def window_stack(x, w_query, w_key, w_value, w_out, num_layers, num_dev):
    rows, dim = x.shape
    blk = rows // 2
    q_heads, head = w_query.shape[2:]
    kv_heads = w_key.shape[2]
    q_width, width = q_heads * head, kv_heads * head
    q_rows, q_ring, kv_rows, kv_ring = dim // 8, 3, dim // 9, 4
    any_ = pl.BlockSpec(memory_space=pl.ANY)
    bf = jnp.bfloat16
    dma, regular = pltpu.SemaphoreType.DMA, pltpu.SemaphoreType.REGULAR
    return pl.pallas_call(
        functools.partial(stack_kernel, num_dev, num_layers),
        in_specs=[any_] * 5,
        out_specs=any_,
        out_shape=jax.ShapeDtypeStruct((rows, dim), bf),
        scratch_shapes=[
            pltpu.VMEM((2, 2, blk, dim), bf),
            pltpu.VMEM((2, blk, dim), bf),
            pltpu.VMEM((6 * blk, 2 * width), bf),
            pltpu.VMEM((blk, dim), bf),
            pltpu.VMEM((2, blk, q_width), bf),
            pltpu.VMEM((dim, q_width), bf),
            pltpu.VMEM((dim, 2 * width), bf),
            pltpu.VMEM((q_width, dim), bf),
            pltpu.VMEM((blk, dim), jnp.float32),
            pltpu.VMEM((q_ring, q_rows, q_heads, head), bf),
            pltpu.VMEM((kv_ring, kv_rows, kv_heads, head), bf),
            pltpu.VMEM((kv_ring, kv_rows, kv_heads, head), bf),
            dma((2,)), dma((2, 2)), dma((2,)), dma((2,)), dma((2,)), dma((2,)),
            regular, regular, dma((2,)), dma((q_ring,)), dma((kv_ring,)), dma((kv_ring,)), dma,
        ],
        compiler_params=pltpu.CompilerParams(vmem_limit_bytes=67043328, collective_id=2, has_side_effects=True),
        cost_estimate=pl.CostEstimate(flops=num_layers * 20 * 10 ** 9, bytes_accessed=num_layers * 28 * 10 ** 6, transcendentals=0),
        name="stack",
    )(x, w_query, w_key, w_value, w_out)


def norm_rows(src, dst):
    rows = src.shape[0]
    step = min(64, rows)

    @pl.loop(0, rows // step)
    def _(i):
        part = pl.ds(pl.multiple_of(i * step, step), step)
        dst[part, :] = normed(src[part, :])


def gather_kernel(num_dev, layer, shift, x_hbm, wq_hbm, wk_hbm, wv_hbm, k_all, v_all, x_all, q_hbm, x_fin,
                  wq_st, wk_st, wv_st, wq_s, wk_s, wv_s, x_s, n_s, k_s, v_s, q_s, wsem, lsem, ssem, send, recv, psend, precv):
    _, rows, dim = x_s.shape
    half = rows // 2
    me = lax.axis_index("cp")
    other = me + 1 - 2 * lax.rem(me, 2)
    near = (lax.rem(me + 2, num_dev), lax.rem(me + num_dev - 2, num_dev))
    hops = num_dev // 4

    def wrap(v):
        return lax.rem(v + 4 * num_dev, num_dev)

    def owner(dev, way, hop):
        if isinstance(way, int):
            return wrap(dev - 2 * hop) if way == 0 else wrap(dev + 2 * hop)
        return wrap(dev + jnp.where(way == 0, -2, 2) * hop)

    def piece(dev, h):
        return x_all.at[dev, pl.ds(h * half, half)]

    def link(way, hop, h):
        ref = piece(owner(me, way, hop - 1), h)
        src = x_hbm.at[pl.ds(h * half, half)] if isinstance(hop, int) and hop == 1 else ref
        return pltpu.make_async_remote_copy(src_ref=src, dst_ref=ref, send_sem=send.at[way, hop, h], recv_sem=recv.at[way, hop, h],
                                            device_id={"cp": near[way]}, device_id_type=MESH)

    def landed(way, hop, h):
        ref = piece(owner(me, way, hop), h)
        return pltpu.make_async_remote_copy(src_ref=ref, dst_ref=ref, send_sem=send.at[way, hop, h], recv_sem=recv.at[way, hop, h],
                                            device_id={"cp": near[way]}, device_id_type=MESH)

    def across(way, hop, h, dev):
        ref = piece(owner(dev, way, hop), h)
        src = x_hbm.at[pl.ds(h * half, half)] if isinstance(hop, int) and hop == 0 else ref
        return pltpu.make_async_remote_copy(src_ref=src, dst_ref=ref, send_sem=psend.at[way, hop, h], recv_sem=precv.at[way, hop, h],
                                            device_id={"cp": other}, device_id_type=MESH)

    wcopies = [pltpu.make_async_copy(w.at[layer], st, wsem.at[i]) for i, (w, st) in enumerate(((wk_hbm, wk_st), (wv_hbm, wv_st), (wq_hbm, wq_st)))]
    for cp in wcopies:
        cp.start()
    first = pltpu.make_async_copy(x_hbm, x_s.at[0], lsem.at[0])
    first.start()
    barrier = pltpu.get_barrier_semaphore()
    for dev in near + (other,):
        pl.semaphore_signal(barrier, inc=1, device_id={"cp": dev}, device_id_type=MESH)
    pl.semaphore_wait(barrier, 3)
    for h in range(2):
        for way in range(2):
            link(way, 1, h).start()
    for h in range(2):
        across(0, 0, h, me).start()
    first.wait()
    keep = pltpu.make_async_copy(x_s.at[0], x_all.at[me], lsem.at[0])
    keep.start()
    keep.wait()
    for cp in wcopies:
        cp.wait()
    step_rows = 256

    @pl.loop(0, dim // step_rows)
    def _(s):
        part = pl.ds(pl.multiple_of(s * step_rows, step_rows), step_rows)
        wk_s[part, :] = wk_st[part].reshape(step_rows, -1)
        wv_s[part, :] = wv_st[part].reshape(step_rows, -1)
        wq_s[part, :] = wq_st[part].reshape(step_rows, -1)

    @pl.loop(0, hops + 1)
    def _(hop):
        for h in range(2):
            for way in range(2):
                last_ok = way == h

                def arrive():
                    with jax.named_scope("land"):
                        landed(way, hop, h).wait_recv()
                    if last_ok:
                        @pl.when(hop < hops)
                        def _():
                            link(way, hop + 1, h).start()
                    else:
                        @pl.when(hop < hops - 1)
                        def _():
                            link(way, hop + 1, h).start()
                    across(way, hop, h, me).start()

                if last_ok:
                    pl.when(hop > 0)(arrive)
                else:
                    pl.when((hop > 0) & (hop < hops))(arrive)

        whole = (hop > 0) & (hop < hops)
        count = jnp.where(whole, 4, 2)

        def source(a):
            mine = a < lax.div(count, 2)
            way = jnp.where(whole, lax.rem(a, 2), 0)
            return mine, way, wrap(jnp.where(mine, me, other) + jnp.where(way == 0, -2, 2) * hop)

        def load(a):
            b = lax.rem(a, 2)
            return pltpu.make_async_copy(x_all.at[source(a)[2]], x_s.at[b], lsem.at[b])

        def stores(a):
            b = lax.rem(a, 2)
            chunk = wrap(source(a)[2] + shift)
            return [pltpu.make_async_copy(t.at[b], o.at[chunk], ssem.at[i, b]) for i, (t, o) in enumerate(((k_s, k_all), (v_s, v_all)))]

        def fetch(a):
            mine, way, _ = source(a)

            @pl.when(jnp.logical_not(mine))
            @scoped("cross")
            def _():
                for h in range(2):
                    across(jnp.where(hop == hops, h, way), hop, h, other).wait_recv()

            load(a).start()

        fetch(0)

        @pl.loop(0, count)
        def _(a):
            b = lax.rem(a, 2)

            @pl.when(a + 1 < count)
            def _():
                fetch(a + 1)

            with jax.named_scope("load"):
                load(a).wait()
            with jax.named_scope("norm"):
                norm_rows(x_s.at[b], n_s)

            @pl.when(a >= 2)
            @scoped("store")
            def _():
                for cp in stores(a - 2):
                    cp.wait()

            with jax.named_scope("keys"):
                k_s[b] = jnp.dot(n_s[...], wk_s[...], preferred_element_type=jnp.float32).astype(jnp.bfloat16)
                v_s[b] = jnp.dot(n_s[...], wv_s[...], preferred_element_type=jnp.float32).astype(jnp.bfloat16)
            for cp in stores(a):
                cp.start()

        for back in range(2):
            for cp in stores(count - 2 + back):
                cp.wait()

    loads = []
    for i, block in enumerate((me, 2 * num_dev - 1 - me)):
        src = wrap(lax.div(block, 2) - shift)
        loads.append(pltpu.make_async_copy(piece(src, lax.rem(block, 2)), x_s.at[0, pl.ds(i * half, half)], lsem.at[i]))
        loads[i].start()
    for cp in loads:
        cp.wait()
    keep = pltpu.make_async_copy(x_s.at[0], x_fin, lsem.at[0])
    keep.start()
    norm_rows(x_s.at[0], n_s)
    with jax.named_scope("query"):
        q_s[...] = jnp.dot(n_s[...], wq_s[...], preferred_element_type=jnp.float32).astype(jnp.bfloat16)
    last = pltpu.make_async_copy(q_s, q_hbm, lsem.at[1])
    last.start()
    last.wait()
    keep.wait()
    for way in range(2):
        for hop in range(1, hops + 1):
            for h in range(2):
                if hop < hops or way == h:
                    link(way, hop, h).wait_send()
                    across(way, hop, h, me).wait_send()
    for h in range(2):
        across(0, 0, h, me).wait_send()


def gather_keys(x, w_query, w_key, w_value, layer, shift, num_dev):
    rows, dim = x.shape
    shapes = [w.shape[2:] for w in (w_query, w_key, w_value)]
    q_width, width = (h * e for h, e in shapes[:2])
    hops = num_dev // 4
    any_ = pl.BlockSpec(memory_space=pl.ANY)
    bf = jnp.bfloat16
    sem = pltpu.SemaphoreType.DMA
    seq = [jax.ShapeDtypeStruct((num_dev, rows, n), bf) for n in (width, width, dim)]
    own = [jax.ShapeDtypeStruct((rows, n), bf) for n in (q_width, dim)]
    return pl.pallas_call(
        functools.partial(gather_kernel, num_dev, layer, shift),
        in_specs=[any_] * 4,
        out_specs=[any_] * 5,
        out_shape=seq + own,
        scratch_shapes=[pltpu.VMEM((dim,) + s, bf) for s in shapes] + [pltpu.VMEM((dim, n), bf) for n in (q_width, width, width)]
        + [pltpu.VMEM((2, rows, dim), bf), pltpu.VMEM((rows, dim), bf)] + [pltpu.VMEM((2, rows, width), bf)] * 2 + [pltpu.VMEM((rows, q_width), bf)]
        + [sem((3,)), sem((2,)), sem((2, 2))] + [sem((2, hops + 1, 2))] * 4,
        compiler_params=params(collective_id=1, has_side_effects=True),
        cost_estimate=pl.CostEstimate(flops=4 * rows * num_dev * dim * width, bytes_accessed=4 * dim * width, transcendentals=0),
        name="gather",
    )(x, w_query, w_key, w_value)


def causal_kernel(layer, seq, blk_ref, q_ref, k_ref, v_ref, x_ref, w_hbm, out_ref, o_s, w_s, upd_s, acc_s, top_s, tot_s, sem):
    g = pl.program_id(0)
    wcopy = pltpu.make_async_copy(w_hbm.at[layer], w_s, sem)

    @pl.when(g == 0)
    def _():
        wcopy.start()

    lead, trail = blk_ref[0], blk_ref[1]
    tile = 4 * BLK
    lanes = tot_s.shape[-1]
    per = tile // BLK
    front = seq // 2 // tile
    num_trail = lax.div(trail + 1 + per - 1, per) - front
    factor = LOG2_E * BLK ** -0.5
    def scores(item):
        _, qrow, t, limit, h = item
        q = q_ref[pl.ds(qrow, BLK), h * BLK:(h + 1) * BLK]
        s = lax.dot_general(q, k_ref[pl.ds(t, tile), :], (((1,), (1,)), ((), ())), preferred_element_type=jnp.float32)
        if limit is not None:
            reach = lax.broadcasted_iota(jnp.int32, (BLK, 1), 0) + limit
            s = jnp.where(lax.broadcasted_iota(jnp.int32, s.shape, 1) <= reach, s, NEG_BIG)
        return s

    def finish(s, item):
        slot, _, t, _, h = item
        top = jnp.max(s, axis=-1, keepdims=True)
        e = jnp.exp2((s - top) * factor)
        tot_s[slot, h] = functools.reduce(jnp.add, [e[:, i * lanes:(i + 1) * lanes] for i in range(tile // lanes)])
        acc_s[slot, h] = jnp.dot(e.astype(jnp.bfloat16), v_ref[pl.ds(t, tile), :], preferred_element_type=jnp.float32)
        top_s[slot, h] = top

    items = []
    for j in range(front + 1):
        late = j < num_trail
        t = jnp.where(late, front + j, j - num_trail) * tile
        second = (front + j, pl.multiple_of(jnp.where(late, BLK, 0), BLK), pl.multiple_of(t, tile), jnp.where(late, trail, lead) * BLK - t)
        for chain in ([(j, BLK, j * tile, None)] if j < front else []) + [second]:
            items += [chain + (h,) for h in range(2)]
    ready = scores(items[0])
    for i, item in enumerate(items):
        now = ready
        if i + 1 < len(items):
            ready = scores(items[i + 1])
        finish(now, item)

    for h in range(2):
        cols = pl.ds(pl.multiple_of(g * 2 * BLK + h * BLK, BLK), BLK)
        for i, slots in enumerate((range(front, 2 * front + 1), range(2 * front + 1))):
            tops = []
            for slot in slots:
                late = slot < front + num_trail
                tops.append(jnp.where(late if i == 1 else jnp.logical_not(late), top_s[slot, h], NEG_BIG))
            new = functools.reduce(jnp.maximum, tops)
            acc = total = None
            for slot, top in zip(slots, tops):
                fix = jnp.exp2((top - new) * factor)
                a, b = acc_s[slot, h] * fix, tot_s[slot, h] * fix
                acc, total = (a, b) if acc is None else (acc + a, total + b)
            o_s[i * BLK:(i + 1) * BLK, cols] = (acc / jnp.sum(total, axis=-1, keepdims=True)).astype(jnp.bfloat16)

    @pl.when(g == pl.num_programs(0) - 1)
    def _():
        wcopy.wait()
        output_rows(o_s, w_s, x_ref, out_ref, upd_s)


def causal_layer(blocks, q, k_all, v_all, x, w_out, layer):
    rows, dim = x.shape
    seq = k_all.shape[0]
    slots = 2 * (seq // 2 // (4 * BLK)) + 1
    kv = pl.BlockSpec((seq, BLK), lambda g, b: (0, g))
    row = pl.BlockSpec((rows, dim), lambda g, b: (0, 0))
    return pl.pallas_call(
        functools.partial(causal_kernel, layer, seq),
        grid_spec=pltpu.PrefetchScalarGridSpec(
            num_scalar_prefetch=1,
            grid=(k_all.shape[1] // BLK,),
            in_specs=[pl.BlockSpec((rows, 2 * BLK), lambda g, b: (0, g)), kv, kv, row, pl.BlockSpec(memory_space=pl.ANY)],
            out_specs=row,
            scratch_shapes=[
                pltpu.VMEM(q.shape, jnp.bfloat16),
                pltpu.VMEM(w_out.shape[1:], jnp.bfloat16),
                pltpu.VMEM((rows, dim), jnp.float32),
                pltpu.VMEM((slots, 2, BLK, BLK), jnp.float32),
                pltpu.VMEM((slots, 2, BLK, 1), jnp.float32),
                pltpu.VMEM((slots, 2, BLK, 128), jnp.float32),
                pltpu.SemaphoreType.DMA,
            ],
        ),
        out_shape=jax.ShapeDtypeStruct((rows, dim), jnp.bfloat16),
        compiler_params=params(),
        cost_estimate=pl.CostEstimate(flops=30 * 10 ** 9, bytes_accessed=2 * w_out[0].size, transcendentals=0),
        name="causal",
    )(blocks, q, k_all, v_all, x, w_out)


def solution(mesh):
    num_dev = mesh.shape["cp"]

    def per_device(hidden, w_query, w_key, w_value, w_out):
        rank = lax.axis_index("cp")
        num_layers = w_query.shape[0]
        rows, dim = hidden.shape
        w_out = w_out.reshape(num_layers, -1, dim)
        last = num_layers - 1
        x = window_stack(hidden, w_query, w_key, w_value, w_out, last, num_dev)
        k_all, v_all, _, q, x_fin = gather_keys(x, w_query, w_key, w_value, last, last, num_dev)
        blocks = jnp.stack([rank, 2 * num_dev - 1 - rank]).astype(jnp.int32)
        return causal_layer(blocks, q, k_all.reshape(-1, k_all.shape[-1]), v_all.reshape(-1, v_all.shape[-1]), x_fin, w_out, last)

    row_spec = P(("dp", "cp"), None)
    return jax.shard_map(per_device, mesh=mesh, in_specs=(row_spec, P(), P(), P(), P()), out_specs=row_spec, check_vma=False)
```

time: 672 us -> 489 us (0.73); the launches traced: 663 us -> 489 us
  Pallas kernels: 582 us -> 488 us
  waiting for transfers between devices: 56.3 us -> 0 us
  starting transfers between devices: 16.1 us -> 0 us
    pallas_call x16 -> x1, Pallas kernels: 311 us -> 219 us  [window_stack(): pl.pallas_call(functools.partial(stack_kernel, num_dev, num_layers), in_s...]
    ppermute x15 -> x0, waiting for transfers between devices: 56.3 us -> none  [the longest x5 56.3 us: per_device(): x_next = lax.ppermute(x, 'cp', ring(-1))]
    ppermute x15 -> x0, starting transfers between devices: 16.1 us -> none  [the longest x5 15.2 us: per_device(): x_next = lax.ppermute(x, 'cp', ring(-1))]
  transfers between devices with their start and end apart: 15 -> 0, of which waited for: 5 -> 0; matrix products, arithmetic and copies ran while one was open for 0% -> 0% of each run, Pallas kernels for 29% -> 0%
where the time goes in v2:
time: 489 us
  Pallas kernels  488 us (100%)
    pallas_call x1, Pallas kernels, gather_keys(): pl.pallas_call(functools.partial(gather_kernel, num_dev, layer, shift), i...  220 us
    pallas_call x1, Pallas kernels, window_stack(): pl.pallas_call(functools.partial(stack_kernel, num_dev, num_layers), in_s...  219 us
    pallas_call x1, Pallas kernels, causal_layer(): pl.pallas_call(functools.partial(causal_kernel, layer, seq), grid_spec=pl...  48.4 us

profile of v2, /device:TPU:21, one launch (start us, length us, event | category | flops | bytes accessed | tf_op | source)
XLA Modules:
  0.0 488.8 jit_solution(14438413975655838789)
XLA Ops:
  0.0 219.4 %stack.13.x_hbm = bf16[512,2304]{1,0:T(8,128)(2,1)} custom-call(bf16[512,2304]{1,0:T(8,128)(2,1)} %x_hbm.1, bf16[6,2304,8,256]{3,2,1,0:T(8,128)(2,1)} %wq_hbm.3, bf16[6,2304,4,256]{3,2,1,0:T(4,128)(2,1)} %wk_hbm.3, bf16[6,2304,4,256]{3,2,1,0:T(4,128)(2,1)} %wv_hbm.3, bf16[6,2048,2304]{2,1,0:T(8,128)(2,1)} %bitcast.5), custom_call_target="tpu_custom_call" | custom-call | flops 99999997952 | bytes 140000000 | tf_op jit(solution)/shard_map/stack/pallas_call | solution.py:390
  219.4 220.2 %gather.1 = (bf16[16,512,1024]{2,1,0:T(8,128)(2,1)}, bf16[16,512,1024]{2,1,0:T(8,128)(2,1)}, bf16[16,512,2304]{2,1,0:T(8,128)(2,1)}, bf16[512,2048]{1,0:T(8,128)(2,1)}, bf16[512,2304]{1,0:T(8,128)(2,1)}) custom-call(bf16[512,2304]{1,0:T(8,128)(2,1)} %stack.13.x_hbm, bf16[6,2304,8,256]{3,2,1,0:T(8,128)(2,1)} %wq_hbm.3, bf16[6,2304,4,256]{3,2,1,0:T(4,128)(2,1)} %wk_hbm.3, ...), custom_call_target="tpu_custom_call" | custom-call | flops 77309411328 | bytes 9437184 | tf_op jit(solution)/shard_map/gather/pallas_call | solution.py:612
  439.6 0.6 pad_add_fusion.blk_ref
  440.2 48.4 %causal.1 = bf16[512,2304]{1,0:T(8,128)(2,1)} custom-call(s32[2]{0:T(128)} %pad_add_fusion.blk_ref, bf16[512,2048]{1,0:T(8,128)(2,1)} %get-tuple-element.9.q_ref, bf16[8192,1024]{1,0:T(8,128)(2,1)} %bitcast.7, bf16[8192,1024]{1,0:T(8,128)(2,1)} %bitcast.8, bf16[512,2304]{1,0:T(8,128)(2,1)} %get-tuple-element.12.x_ref, bf16[6,2048,2304]{2,1,0:T(8,128)(2,1)} %bitcast.6), custom_call_target="tpu_custom_call" | custom-call | flops 30000001024 | bytes 9437184 | tf_op jit(solution)/shard_map/causal/pallas_call | solution.py:699

commit v3 on v2

--- a/solution.py
+++ b/solution.py
@@ -53,9 +53,9 @@
     return wrap
 
 
-def stack_kernel(num_dev, num_layers, x_hbm, wq_hbm, wk_hbm, wv_hbm, wo_hbm, out_hbm,
+def stack_kernel(num_dev, num_layers, x_hbm, wq_hbm, wk_hbm, wv_hbm, wo_hbm, x_all,
                  xr, xn, kv, n_s, q_s, wq_s, wkv_s, wo_s, upd_s, stq, stk, stv,
-                 x_send, x_recv, h_send, h_recv, c_send, c_recv, h_free, c_free, xsem, qsem, ksem, vsem, wsem):
+                 g_send, g_recv, x_send, x_recv, h_send, h_recv, c_send, c_recv, h_free, c_free, xsem, qsem, ksem, vsem, wsem):
     blk, dim = n_s.shape
     width = wkv_s.shape[1] // 2
     heads = q_s.shape[2] // width
@@ -68,6 +68,10 @@
     is_odd, is_even = odd == 1, odd == 0
     left, right = lax.rem(me + num_dev - 1, num_dev), lax.rem(me + 1, num_dev)
 
+    other = jnp.where(is_odd, left, right)
+    peers = (lax.rem(me + 2, num_dev), lax.rem(me + num_dev - 2, num_dev), other)
+    sources = (peers[1], peers[0], other)
+
     def block(i):
         return pl.ds(pl.multiple_of(i * blk, blk), blk)
 
@@ -76,6 +80,12 @@
 
     def x_copy(slot, s):
         return remote(xn.at[s], xr.at[slot, s], x_send.at[s], x_recv.at[slot, s], left)
+
+    def g_copy(i, owner):
+        return remote(xn.at[0], x_all.at[owner, block(0)], g_send.at[i], g_recv.at[i], peers[i])
+
+    def keep(s):
+        return pltpu.make_async_copy(xn.at[s], x_all.at[me, block(s)], xsem.at[s])
 
     def h_copy(s):
         return remote(kv.at[block(2 + s)], kv.at[block(s)], h_send.at[s], h_recv.at[s], right)
@@ -199,9 +209,9 @@
     for i in range(q_ring):
         q_stage(0, i).start()
     barrier = pltpu.get_barrier_semaphore()
-    for dev in (left, right):
+    for dev in (left, right) + peers[:2]:
         signal(barrier, dev)
-    pl.semaphore_wait(barrier, 2)
+    pl.semaphore_wait(barrier, 4)
     for s in range(2):
         loads[s].wait()
         x_copy(0, s).start()
@@ -236,12 +246,6 @@
             @pl.loop(0, 2)
             @scoped("own")
             def _(j):
-                per = q_parts // 4
-                first = (2 * s + j) * per
-                for t in range(per):
-                    q_stage(layer, first + t).wait()
-                    q_flat(layer, first + t)
-                    q_next(layer, first + t)
                 cols = pl.ds(pl.multiple_of(j * tile, tile), tile)
                 kv[block(2 + s), cols] = dot(wkv_s[:, cols])
 
@@ -259,6 +263,13 @@
             @pl.when(is_odd)
             def _():
                 c_copy(s).start()
+
+        @pl.loop(0, q_parts)
+        @scoped("q_lay")
+        def _(i):
+            q_stage(layer, i).wait()
+            q_flat(layer, i)
+            q_next(layer, i)
 
         wo_copy(layer).start()
 
@@ -365,16 +376,25 @@
 
             @pl.when(jnp.logical_not(more))
             def _():
-                pltpu.make_async_copy(xn.at[s], out_hbm.at[block(s)], xsem.at[s]).start()
+                keep(s).start()
+
+                @pl.when(s == 0)
+                def _():
+                    for i in range(3):
+                        g_copy(i, me).start()
 
     for s in range(2):
         h_copy(s).wait_send()
-        pltpu.make_async_copy(xn.at[s], out_hbm.at[block(s)], xsem.at[s]).wait()
+        keep(s).wait()
 
     @pl.when(is_odd)
     def _():
         for s in range(2):
             c_copy(s).wait_send()
+
+    for i in range(3):
+        g_copy(i, me).wait_send()
+        g_copy(i, sources[i]).wait_recv()
 
 
 def window_stack(x, w_query, w_key, w_value, w_out, num_layers, num_dev):
@@ -383,7 +403,7 @@
     q_heads, head = w_query.shape[2:]
     kv_heads = w_key.shape[2]
     q_width, width = q_heads * head, kv_heads * head
-    q_rows, q_ring, kv_rows, kv_ring = dim // 8, 3, dim // 9, 4
+    q_rows, q_ring, kv_rows, kv_ring = dim // 8, 4, dim // 9, 4
     any_ = pl.BlockSpec(memory_space=pl.ANY)
     bf = jnp.bfloat16
     dma, regular = pltpu.SemaphoreType.DMA, pltpu.SemaphoreType.REGULAR
@@ -391,7 +411,7 @@
         functools.partial(stack_kernel, num_dev, num_layers),
         in_specs=[any_] * 5,
         out_specs=any_,
-        out_shape=jax.ShapeDtypeStruct((rows, dim), bf),
+        out_shape=jax.ShapeDtypeStruct((num_dev, rows, dim), bf),
         scratch_shapes=[
             pltpu.VMEM((2, 2, blk, dim), bf),
             pltpu.VMEM((2, blk, dim), bf),
@@ -405,7 +425,7 @@
             pltpu.VMEM((q_ring, q_rows, q_heads, head), bf),
             pltpu.VMEM((kv_ring, kv_rows, kv_heads, head), bf),
             pltpu.VMEM((kv_ring, kv_rows, kv_heads, head), bf),
-            dma((2,)), dma((2, 2)), dma((2,)), dma((2,)), dma((2,)), dma((2,)),
+            dma((3,)), dma((3,)), dma((2,)), dma((2, 2)), dma((2,)), dma((2,)), dma((2,)), dma((2,)),
             regular, regular, dma((2,)), dma((q_ring,)), dma((kv_ring,)), dma((kv_ring,)), dma,
         ],
         compiler_params=pltpu.CompilerParams(vmem_limit_bytes=67043328, collective_id=2, has_side_effects=True),
@@ -424,8 +444,8 @@
         dst[part, :] = normed(src[part, :])
 
 
-def gather_kernel(num_dev, layer, shift, x_hbm, wq_hbm, wk_hbm, wv_hbm, k_all, v_all, x_all, q_hbm, x_fin,
-                  wq_st, wk_st, wv_st, wq_s, wk_s, wv_s, x_s, n_s, k_s, v_s, q_s, wsem, lsem, ssem, send, recv, psend, precv):
+def gather_kernel(num_dev, layer, shift, x_in, wq_hbm, wk_hbm, wv_hbm, k_all, v_all, x_all, q_hbm, x_fin,
+                  wq_st, wk_st, wv_st, wq_s, wk_s, wv_s, x_s, n_s, k_s, v_s, q_s, f_s, wsem, fsem, lsem, ssem, send, recv, psend, precv):
     _, rows, dim = x_s.shape
     half = rows // 2
     me = lax.axis_index("cp")
@@ -446,8 +466,7 @@
 
     def link(way, hop, h):
         ref = piece(owner(me, way, hop - 1), h)
-        src = x_hbm.at[pl.ds(h * half, half)] if isinstance(hop, int) and hop == 1 else ref
-        return pltpu.make_async_remote_copy(src_ref=src, dst_ref=ref, send_sem=send.at[way, hop, h], recv_sem=recv.at[way, hop, h],
+        return pltpu.make_async_remote_copy(src_ref=ref, dst_ref=ref, send_sem=send.at[way, hop, h], recv_sem=recv.at[way, hop, h],
                                             device_id={"cp": near[way]}, device_id_type=MESH)
 
     def landed(way, hop, h):
@@ -457,28 +476,29 @@
 
     def across(way, hop, h, dev):
         ref = piece(owner(dev, way, hop), h)
-        src = x_hbm.at[pl.ds(h * half, half)] if isinstance(hop, int) and hop == 0 else ref
-        return pltpu.make_async_remote_copy(src_ref=src, dst_ref=ref, send_sem=psend.at[way, hop, h], recv_sem=precv.at[way, hop, h],
+        return pltpu.make_async_remote_copy(src_ref=ref, dst_ref=ref, send_sem=psend.at[way, hop, h], recv_sem=precv.at[way, hop, h],
                                             device_id={"cp": other}, device_id_type=MESH)
+
+    def finals():
+        copies = []
+        for i, block in enumerate((me, 2 * num_dev - 1 - me)):
+            src = wrap(lax.div(block, 2) - shift)
+            copies.append(pltpu.make_async_copy(piece(src, lax.rem(block, 2)), f_s.at[pl.ds(i * half, half)], fsem.at[i]))
+        return copies
 
     wcopies = [pltpu.make_async_copy(w.at[layer], st, wsem.at[i]) for i, (w, st) in enumerate(((wk_hbm, wk_st), (wv_hbm, wv_st), (wq_hbm, wq_st)))]
     for cp in wcopies:
         cp.start()
-    first = pltpu.make_async_copy(x_hbm, x_s.at[0], lsem.at[0])
-    first.start()
     barrier = pltpu.get_barrier_semaphore()
     for dev in near + (other,):
         pl.semaphore_signal(barrier, inc=1, device_id={"cp": dev}, device_id_type=MESH)
     pl.semaphore_wait(barrier, 3)
-    for h in range(2):
-        for way in range(2):
-            link(way, 1, h).start()
-    for h in range(2):
-        across(0, 0, h, me).start()
-    first.wait()
-    keep = pltpu.make_async_copy(x_s.at[0], x_all.at[me], lsem.at[0])
-    keep.start()
-    keep.wait()
+    for way in range(2):
+        link(way, 1, 1).start()
+    across(0, 0, 1, me).start()
+    for way in range(2):
+        link(way, 2, 0).start()
+        across(way, 1, 0, me).start()
     for cp in wcopies:
         cp.wait()
     step_rows = 256
@@ -509,10 +529,11 @@
                             link(way, hop + 1, h).start()
                     across(way, hop, h, me).start()
 
+                first_hop = 2 - h
                 if last_ok:
-                    pl.when(hop > 0)(arrive)
+                    pl.when(hop >= first_hop)(arrive)
                 else:
-                    pl.when((hop > 0) & (hop < hops))(arrive)
+                    pl.when((hop >= first_hop) & (hop < hops))(arrive)
 
         whole = (hop > 0) & (hop < hops)
         count = jnp.where(whole, 4, 2)
@@ -537,8 +558,11 @@
             @pl.when(jnp.logical_not(mine))
             @scoped("cross")
             def _():
-                for h in range(2):
-                    across(jnp.where(hop == hops, h, way), hop, h, other).wait_recv()
+                @pl.when(hop > 0)
+                def _():
+                    across(jnp.where(hop == hops, 0, way), hop, 0, other).wait_recv()
+
+                across(jnp.where(hop == hops, 1, way), hop, 1, other).wait_recv()
 
             load(a).start()
 
@@ -547,15 +571,20 @@
         @pl.loop(0, count)
         def _(a):
             b = lax.rem(a, 2)
-
-            @pl.when(a + 1 < count)
-            def _():
-                fetch(a + 1)
 
             with jax.named_scope("load"):
                 load(a).wait()
             with jax.named_scope("norm"):
                 norm_rows(x_s.at[b], n_s)
+
+            @pl.when(a + 1 < count)
+            def _():
+                fetch(a + 1)
+
+            @pl.when((hop == hops) & (a == 0))
+            def _():
+                for cp in finals():
+                    cp.start()
 
             @pl.when(a >= 2)
             @scoped("store")
@@ -573,16 +602,11 @@
             for cp in stores(count - 2 + back):
                 cp.wait()
 
-    loads = []
-    for i, block in enumerate((me, 2 * num_dev - 1 - me)):
-        src = wrap(lax.div(block, 2) - shift)
-        loads.append(pltpu.make_async_copy(piece(src, lax.rem(block, 2)), x_s.at[0, pl.ds(i * half, half)], lsem.at[i]))
-        loads[i].start()
-    for cp in loads:
+    for cp in finals():
         cp.wait()
-    keep = pltpu.make_async_copy(x_s.at[0], x_fin, lsem.at[0])
+    keep = pltpu.make_async_copy(f_s, x_fin, lsem.at[0])
     keep.start()
-    norm_rows(x_s.at[0], n_s)
+    norm_rows(f_s, n_s)
     with jax.named_scope("query"):
         q_s[...] = jnp.dot(n_s[...], wq_s[...], preferred_element_type=jnp.float32).astype(jnp.bfloat16)
     last = pltpu.make_async_copy(q_s, q_hbm, lsem.at[1])
@@ -593,14 +617,14 @@
         for hop in range(1, hops + 1):
             for h in range(2):
                 if hop < hops or way == h:
-                    link(way, hop, h).wait_send()
                     across(way, hop, h, me).wait_send()
-    for h in range(2):
-        across(0, 0, h, me).wait_send()
-
-
-def gather_keys(x, w_query, w_key, w_value, layer, shift, num_dev):
-    rows, dim = x.shape
+                    if hop + h > 1:
+                        link(way, hop, h).wait_send()
+    across(0, 0, 1, me).wait_send()
+
+
+def gather_keys(x_all, w_query, w_key, w_value, layer, shift, num_dev):
+    _, rows, dim = x_all.shape
     shapes = [w.shape[2:] for w in (w_query, w_key, w_value)]
     q_width, width = (h * e for h, e in shapes[:2])
     hops = num_dev // 4
@@ -614,13 +638,14 @@
         in_specs=[any_] * 4,
         out_specs=[any_] * 5,
         out_shape=seq + own,
+        input_output_aliases={0: 2},
         scratch_shapes=[pltpu.VMEM((dim,) + s, bf) for s in shapes] + [pltpu.VMEM((dim, n), bf) for n in (q_width, width, width)]
-        + [pltpu.VMEM((2, rows, dim), bf), pltpu.VMEM((rows, dim), bf)] + [pltpu.VMEM((2, rows, width), bf)] * 2 + [pltpu.VMEM((rows, q_width), bf)]
-        + [sem((3,)), sem((2,)), sem((2, 2))] + [sem((2, hops + 1, 2))] * 4,
+        + [pltpu.VMEM((2, rows, dim), bf), pltpu.VMEM((rows, dim), bf)] + [pltpu.VMEM((2, rows, width), bf)] * 2 + [pltpu.VMEM((rows, q_width), bf), pltpu.VMEM((rows, dim), bf)]
+        + [sem((3,)), sem((2,)), sem((2,)), sem((2, 2))] + [sem((2, hops + 1, 2))] * 4,
         compiler_params=params(collective_id=1, has_side_effects=True),
         cost_estimate=pl.CostEstimate(flops=4 * rows * num_dev * dim * width, bytes_accessed=4 * dim * width, transcendentals=0),
         name="gather",
-    )(x, w_query, w_key, w_value)
+    )(x_all, w_query, w_key, w_value)
 
 
 def causal_kernel(layer, seq, blk_ref, q_ref, k_ref, v_ref, x_ref, w_hbm, out_ref, o_s, w_s, upd_s, acc_s, top_s, tot_s, sem):
@@ -656,11 +681,17 @@
         top_s[slot, h] = top
 
     items = []
-    for j in range(front + 1):
-        late = j < num_trail
-        t = jnp.where(late, front + j, j - num_trail) * tile
-        second = (front + j, pl.multiple_of(jnp.where(late, BLK, 0), BLK), pl.multiple_of(t, tile), jnp.where(late, trail, lead) * BLK - t)
-        for chain in ([(j, BLK, j * tile, None)] if j < front else []) + [second]:
+    for j in range(front):
+        chains = [(j, BLK, j * tile, None)]
+        if j < 2:
+            block, t = ((trail, front + num_trail - 1), (lead, front - num_trail))[j]
+            t = pl.multiple_of(t * tile, tile)
+            chains.append((front + j, (1 - j) * BLK, t, block * BLK - t))
+        if j > 0:
+            late = j < num_trail
+            t = jnp.where(late, front + j - 1, j - num_trail) * tile
+            chains.append((front + 1 + j, pl.multiple_of(jnp.where(late, BLK, 0), BLK), pl.multiple_of(t, tile), None))
+        for chain in chains:
             items += [chain + (h,) for h in range(2)]
     ready = scores(items[0])
     for i, item in enumerate(items):
@@ -671,11 +702,15 @@
 
     for h in range(2):
         cols = pl.ds(pl.multiple_of(g * 2 * BLK + h * BLK, BLK), BLK)
-        for i, slots in enumerate((range(front, 2 * front + 1), range(2 * front + 1))):
+        shared = range(front + 2, 2 * front + 1)
+        for i, slots in enumerate(([front + 1, *shared], [*range(front + 1), *shared])):
             tops = []
             for slot in slots:
-                late = slot < front + num_trail
-                tops.append(jnp.where(late if i == 1 else jnp.logical_not(late), top_s[slot, h], NEG_BIG))
+                top = top_s[slot, h]
+                if slot > front + 1:
+                    late = slot - front - 1 < num_trail
+                    top = jnp.where(late if i == 1 else jnp.logical_not(late), top, NEG_BIG)
+                tops.append(top)
             new = functools.reduce(jnp.maximum, tops)
             acc = total = None
             for slot, top in zip(slots, tops):

time: 489 us -> 463 us (0.947)
  Pallas kernels: 488 us -> 462 us
    pallas_call x1, Pallas kernels: 220 us -> 193 us  [gather_keys(): pl.pallas_call(functools.partial(gather_kernel, num_dev, layer, shift), i...]
    pallas_call x1, Pallas kernels: 219 us -> 224 us  [window_stack(): pl.pallas_call(functools.partial(stack_kernel, num_dev, num_layers), in_s...]
where the time goes in v3:
time: 463 us
  Pallas kernels  462 us (100%)
    pallas_call x1, Pallas kernels, window_stack(): pl.pallas_call(functools.partial(stack_kernel, num_dev, num_layers), in_s...  224 us
    pallas_call x1, Pallas kernels, gather_keys(): pl.pallas_call(functools.partial(gather_kernel, num_dev, layer, shift), i...  193 us
    pallas_call x1, Pallas kernels, causal_layer(): pl.pallas_call(functools.partial(causal_kernel, layer, seq), grid_spec=pl...  44.7 us

profile of v3, /device:TPU:21, one launch (start us, length us, event | category | flops | bytes accessed | tf_op | source)
XLA Modules:
  0.0 463.0 jit_solution(15039477141445675500)
XLA Ops:
  0.0 224.4 %stack.13.x_in = bf16[16,512,2304]{2,1,0:T(8,128)(2,1)} custom-call(bf16[512,2304]{1,0:T(8,128)(2,1)} %x_hbm.1, bf16[6,2304,8,256]{3,2,1,0:T(8,128)(2,1)} %wq_hbm.3, bf16[6,2304,4,256]{3,2,1,0:T(4,128)(2,1)} %wk_hbm.3, bf16[6,2304,4,256]{3,2,1,0:T(4,128)(2,1)} %wv_hbm.3, bf16[6,2048,2304]{2,1,0:T(8,128)(2,1)} %bitcast.5), custom_call_target="tpu_custom_call" | custom-call | flops 99999997952 | bytes 140000000 | tf_op jit(solution)/shard_map/stack/pallas_call | solution.py:410
  224.5 193.1 %gather.1 = (bf16[16,512,1024]{2,1,0:T(8,128)(2,1)}, bf16[16,512,1024]{2,1,0:T(8,128)(2,1)}, bf16[16,512,2304]{2,1,0:T(8,128)(2,1)}, bf16[512,2048]{1,0:T(8,128)(2,1)}, bf16[512,2304]{1,0:T(8,128)(2,1)}) custom-call(bf16[16,512,2304]{2,1,0:T(8,128)(2,1)} %stack.13.x_in, bf16[6,2304,8,256]{3,2,1,0:T(8,128)(2,1)} %wq_hbm.3, ...), custom_call_target="tpu_custom_call", output_to_operand_aliasing={{2}: (0, {})} | custom-call | flops 77309411328 | bytes 9437184 | tf_op jit(solution)/shard_map/gather/pallas_call | solution.py:636
  417.6 0.6 pad_add_fusion.blk_ref
  418.2 44.7 %causal.1 = bf16[512,2304]{1,0:T(8,128)(2,1)} custom-call(s32[2]{0:T(128)} %pad_add_fusion.blk_ref, bf16[512,2048]{1,0:T(8,128)(2,1)} %get-tuple-element.9.q_ref, bf16[8192,1024]{1,0:T(8,128)(2,1)} %bitcast.7, bf16[8192,1024]{1,0:T(8,128)(2,1)} %bitcast.8, bf16[512,2304]{1,0:T(8,128)(2,1)} %get-tuple-element.12.x_ref, bf16[6,2048,2304]{2,1,0:T(8,128)(2,1)} %bitcast.6), custom_call_target="tpu_custom_call" | custom-call | flops 30000001024 | bytes 9437184 | tf_op jit(solution)/shard_map/causal/pallas_call | solution.py:734

commit v4 on v3

--- a/solution.py
+++ b/solution.py
@@ -34,9 +34,9 @@
         cols = pl.ds(pl.multiple_of(s * tile, tile), tile)
         upd_s[:, cols] = jnp.dot(o_s[...], w_s[:, cols], preferred_element_type=jnp.float32)
 
-    @pl.loop(0, rows // 64)
+    @pl.loop(0, rows // 16, unroll=16)
     def _(s):
-        part = pl.ds(pl.multiple_of(s * 64, 64), 64)
+        part = pl.ds(pl.multiple_of(s * 16, 16), 16)
         upd = upd_s[part, :]
         scale = lax.rsqrt(jnp.mean(upd * upd, axis=-1, keepdims=True) + EPS_NORM)
         out_ref[part, :] = (x_ref[part, :].astype(jnp.float32) + upd * scale).astype(jnp.bfloat16)
@@ -87,8 +87,9 @@
     def keep(s):
         return pltpu.make_async_copy(xn.at[s], x_all.at[me, block(s)], xsem.at[s])
 
-    def h_copy(s):
-        return remote(kv.at[block(2 + s)], kv.at[block(s)], h_send.at[s], h_recv.at[s], right)
+    def h_copy(s, j):
+        cols = pl.ds(pl.multiple_of(j * width, width), width)
+        return remote(kv.at[block(2 + s), cols], kv.at[block(s), cols], h_send.at[s, j], h_recv.at[s, j], right)
 
     def c_copy(s):
         return remote(kv.at[block(2 + s)], kv.at[block(4 + s)], c_send.at[s], c_recv.at[s], left)
@@ -144,9 +145,9 @@
         return pltpu.make_async_copy(wo_hbm.at[layer], wo_s, wsem)
 
     def norm_into(ref):
-        step = min(64, blk)
-
-        @pl.loop(0, blk // step)
+        step = min(16, blk)
+
+        @pl.loop(0, blk // step, unroll=blk // step)
         def _(i):
             part = pl.ds(pl.multiple_of(i * step, step), step)
             n_s[part, :] = normed(ref[part, :])
@@ -231,7 +232,8 @@
         @pl.when(layer > 0)
         def _():
             for s in range(2):
-                h_copy(s).wait_send()
+                for j in range(2):
+                    h_copy(s, j).wait_send()
 
             @pl.when(is_odd)
             def _():
@@ -249,16 +251,15 @@
                 cols = pl.ds(pl.multiple_of(j * tile, tile), tile)
                 kv[block(2 + s), cols] = dot(wkv_s[:, cols])
 
-            @pl.when((layer > 0) & (s == 0))
-            @scoped("credit")
-            def _():
-                pl.semaphore_wait(h_free, 1)
-
-                @pl.when(is_odd)
+                @pl.when((layer > 0) & (s == 0) & (j == 0))
                 def _():
-                    pl.semaphore_wait(c_free, 1)
-
-            h_copy(s).start()
+                    pl.semaphore_wait(h_free, 1)
+
+                    @pl.when(is_odd)
+                    def _():
+                        pl.semaphore_wait(c_free, 1)
+
+                h_copy(s, j).start()
 
             @pl.when(is_odd)
             def _():
@@ -305,7 +306,8 @@
             @scoped("h_wait")
             def _():
                 for i in range(2):
-                    h_copy(i).wait_recv()
+                    for j in range(2):
+                        h_copy(i, j).wait_recv()
 
             @pl.when(is_even)
             @scoped("c_wait")
@@ -360,10 +362,9 @@
 
             with jax.named_scope("x_sent"):
                 x_copy(slot, s).wait_send()
-            step = min(64, blk)
-
-            @pl.loop(0, blk // step)
-            @scoped("resid")
+            step = min(16, blk)
+
+            @pl.loop(0, blk // step, unroll=blk // step)
             def _(i):
                 part = pl.ds(pl.multiple_of(i * step, step), step)
                 upd = upd_s[part, :]
@@ -384,7 +385,8 @@
                         g_copy(i, me).start()
 
     for s in range(2):
-        h_copy(s).wait_send()
+        for j in range(2):
+            h_copy(s, j).wait_send()
         keep(s).wait()
 
     @pl.when(is_odd)
@@ -425,7 +427,7 @@
             pltpu.VMEM((q_ring, q_rows, q_heads, head), bf),
             pltpu.VMEM((kv_ring, kv_rows, kv_heads, head), bf),
             pltpu.VMEM((kv_ring, kv_rows, kv_heads, head), bf),
-            dma((3,)), dma((3,)), dma((2,)), dma((2, 2)), dma((2,)), dma((2,)), dma((2,)), dma((2,)),
+            dma((3,)), dma((3,)), dma((2,)), dma((2, 2)), dma((2, 2)), dma((2, 2)), dma((2,)), dma((2,)),
             regular, regular, dma((2,)), dma((q_ring,)), dma((kv_ring,)), dma((kv_ring,)), dma,
         ],
         compiler_params=pltpu.CompilerParams(vmem_limit_bytes=67043328, collective_id=2, has_side_effects=True),
@@ -436,16 +438,16 @@
 
 def norm_rows(src, dst):
     rows = src.shape[0]
-    step = min(64, rows)
-
-    @pl.loop(0, rows // step)
+    step = min(16, rows)
+
+    @pl.loop(0, rows // step, unroll=min(16, rows // step))
     def _(i):
         part = pl.ds(pl.multiple_of(i * step, step), step)
         dst[part, :] = normed(src[part, :])
 
 
 def gather_kernel(num_dev, layer, shift, x_in, wq_hbm, wk_hbm, wv_hbm, k_all, v_all, x_all, q_hbm, x_fin,
-                  wq_st, wk_st, wv_st, wq_s, wk_s, wv_s, x_s, n_s, k_s, v_s, q_s, f_s, wsem, fsem, lsem, ssem, send, recv, psend, precv):
+                  wq_st, wk_st, wv_st, wq_s, wk_s, wv_s, x_s, n_s, k_s, v_s, q_s, f_s, wsem, fsem, lsem, ssem, send, recv, psend, precv, csend, crecv):
     _, rows, dim = x_s.shape
     half = rows // 2
     me = lax.axis_index("cp")
@@ -477,6 +479,13 @@
     def across(way, hop, h, dev):
         ref = piece(owner(dev, way, hop), h)
         return pltpu.make_async_remote_copy(src_ref=ref, dst_ref=ref, send_sem=psend.at[way, hop, h], recv_sem=precv.at[way, hop, h],
+                                            device_id={"cp": other}, device_id_type=MESH)
+
+    crossings = [(0, 0, 1)] + [(way, hop, h) for hop in range(1, hops + 1) for way in range(2) for h in range(2) if hop < hops or way == h]
+
+    def share(i, a, hop, chunk):
+        src, dst = ((k_s, k_all), (v_s, v_all))[i]
+        return pltpu.make_async_remote_copy(src_ref=src.at[a], dst_ref=dst.at[chunk], send_sem=csend.at[i, a], recv_sem=crecv.at[i, a, hop],
                                             device_id={"cp": other}, device_id_type=MESH)
 
     def finals():
@@ -536,71 +545,61 @@
                     pl.when((hop >= first_hop) & (hop < hops))(arrive)
 
         whole = (hop > 0) & (hop < hops)
-        count = jnp.where(whole, 4, 2)
+        count = jnp.where(whole, 2, 1)
 
         def source(a):
-            mine = a < lax.div(count, 2)
-            way = jnp.where(whole, lax.rem(a, 2), 0)
-            return mine, way, wrap(jnp.where(mine, me, other) + jnp.where(way == 0, -2, 2) * hop)
+            return wrap(me + jnp.where(a == 0, -2, 2) * hop)
 
         def load(a):
-            b = lax.rem(a, 2)
-            return pltpu.make_async_copy(x_all.at[source(a)[2]], x_s.at[b], lsem.at[b])
-
-        def stores(a):
-            b = lax.rem(a, 2)
-            chunk = wrap(source(a)[2] + shift)
-            return [pltpu.make_async_copy(t.at[b], o.at[chunk], ssem.at[i, b]) for i, (t, o) in enumerate(((k_s, k_all), (v_s, v_all)))]
-
-        def fetch(a):
-            mine, way, _ = source(a)
-
-            @pl.when(jnp.logical_not(mine))
-            @scoped("cross")
-            def _():
-                @pl.when(hop > 0)
-                def _():
-                    across(jnp.where(hop == hops, 0, way), hop, 0, other).wait_recv()
-
-                across(jnp.where(hop == hops, 1, way), hop, 1, other).wait_recv()
-
-            load(a).start()
-
-        fetch(0)
+            return pltpu.make_async_copy(x_all.at[source(a)], x_s.at[a], lsem.at[a])
+
+        load(0).start()
 
         @pl.loop(0, count)
         def _(a):
-            b = lax.rem(a, 2)
-
             with jax.named_scope("load"):
                 load(a).wait()
+
+            @pl.when(a + 1 < count)
+            def _():
+                load(a + 1).start()
+
             with jax.named_scope("norm"):
-                norm_rows(x_s.at[b], n_s)
-
-            @pl.when(a + 1 < count)
-            def _():
-                fetch(a + 1)
-
-            @pl.when((hop == hops) & (a == 0))
-            def _():
+                norm_rows(x_s.at[a], n_s)
+            chunk = wrap(source(a) + shift)
+
+            def keep(i):
+                src, dst = ((k_s, k_all), (v_s, v_all))[i]
+                return pltpu.make_async_copy(src.at[a], dst.at[chunk], ssem.at[i, a])
+
+            with jax.named_scope("keys"):
+                k_s[a] = jnp.dot(n_s[...], wk_s[...], preferred_element_type=jnp.float32).astype(jnp.bfloat16)
+            keep(0).start()
+            share(0, a, hop, chunk).start()
+
+            @pl.when(hop == hops)
+            @scoped("cross")
+            def _():
+                for way, far, h in crossings:
+                    across(way, far, h, other).wait_recv()
                 for cp in finals():
                     cp.start()
 
-            @pl.when(a >= 2)
-            @scoped("store")
-            def _():
-                for cp in stores(a - 2):
-                    cp.wait()
-
             with jax.named_scope("keys"):
-                k_s[b] = jnp.dot(n_s[...], wk_s[...], preferred_element_type=jnp.float32).astype(jnp.bfloat16)
-                v_s[b] = jnp.dot(n_s[...], wv_s[...], preferred_element_type=jnp.float32).astype(jnp.bfloat16)
-            for cp in stores(a):
-                cp.start()
-
-        for back in range(2):
-            for cp in stores(count - 2 + back):
-                cp.wait()
+                v_s[a] = jnp.dot(n_s[...], wv_s[...], preferred_element_type=jnp.float32).astype(jnp.bfloat16)
+            keep(1).start()
+            share(1, a, hop, chunk).start()
+
+        @pl.loop(0, count)
+        def _(a):
+            for i in range(2):
+                src, dst = ((k_s, k_all), (v_s, v_all))[i]
+                pltpu.make_async_copy(src.at[a], dst.at[wrap(source(a) + shift)], ssem.at[i, a]).wait()
+
+                @pl.when(hop < hops)
+                @scoped("shared")
+                def _():
+                    share(i, a, hop, wrap(source(a) + shift)).wait_send()
 
     for cp in finals():
         cp.wait()
@@ -613,14 +612,15 @@
     last.start()
     last.wait()
     keep.wait()
-    for way in range(2):
-        for hop in range(1, hops + 1):
-            for h in range(2):
-                if hop < hops or way == h:
-                    across(way, hop, h, me).wait_send()
-                    if hop + h > 1:
-                        link(way, hop, h).wait_send()
-    across(0, 0, 1, me).wait_send()
+    for i in range(2):
+        share(i, 0, hops, wrap(me + shift)).wait_send()
+        for hop in range(hops + 1):
+            for way in range(2 if 0 < hop < hops else 1):
+                share(i, way, hop, wrap(owner(other, way, hop) + shift)).wait_recv()
+    for way, hop, h in crossings:
+        across(way, hop, h, me).wait_send()
+        if hop + h > 1:
+            link(way, hop, h).wait_send()
 
 
 def gather_keys(x_all, w_query, w_key, w_value, layer, shift, num_dev):
@@ -641,7 +641,7 @@
         input_output_aliases={0: 2},
         scratch_shapes=[pltpu.VMEM((dim,) + s, bf) for s in shapes] + [pltpu.VMEM((dim, n), bf) for n in (q_width, width, width)]
         + [pltpu.VMEM((2, rows, dim), bf), pltpu.VMEM((rows, dim), bf)] + [pltpu.VMEM((2, rows, width), bf)] * 2 + [pltpu.VMEM((rows, q_width), bf), pltpu.VMEM((rows, dim), bf)]
-        + [sem((3,)), sem((2,)), sem((2,)), sem((2, 2))] + [sem((2, hops + 1, 2))] * 4,
+        + [sem((3,)), sem((2,)), sem((2,)), sem((2, 2))] + [sem((2, hops + 1, 2))] * 4 + [sem((2, 2)), sem((2, 2, hops + 1))],
         compiler_params=params(collective_id=1, has_side_effects=True),
         cost_estimate=pl.CostEstimate(flops=4 * rows * num_dev * dim * width, bytes_accessed=4 * dim * width, transcendentals=0),
         name="gather",

time: 463 us -> 444 us (0.959)
  Pallas kernels: 462 us -> 443 us
    pallas_call x1, Pallas kernels: 193 us -> 181 us  [gather_keys(): pl.pallas_call(functools.partial(gather_kernel, num_dev, layer, shift), i...]
    pallas_call x1, Pallas kernels: 224 us -> 217 us  [window_stack(): pl.pallas_call(functools.partial(stack_kernel, num_dev, num_layers), in_s...]
where the time goes in v4:
time: 444 us; the launch traced here: 443 us
  Pallas kernels  443 us (100%)
    pallas_call x1, Pallas kernels, window_stack(): pl.pallas_call(functools.partial(stack_kernel, num_dev, num_layers), in_s...  217 us
    pallas_call x1, Pallas kernels, gather_keys(): pl.pallas_call(functools.partial(gather_kernel, num_dev, layer, shift), i...  181 us
    pallas_call x1, Pallas kernels, causal_layer(): pl.pallas_call(functools.partial(causal_kernel, layer, seq), grid_spec=pl...  45.3 us

profile of v4, /device:TPU:21, one launch (start us, length us, event | category | flops | bytes accessed | tf_op | source)
XLA Modules:
  0.0 443.4 jit_solution(5180523206271371231)
XLA Ops:
  0.0 216.7 %stack.13.x_in = bf16[16,512,2304]{2,1,0:T(8,128)(2,1)} custom-call(bf16[512,2304]{1,0:T(8,128)(2,1)} %x_hbm.1, bf16[6,2304,8,256]{3,2,1,0:T(8,128)(2,1)} %wq_hbm.3, bf16[6,2304,4,256]{3,2,1,0:T(4,128)(2,1)} %wk_hbm.3, bf16[6,2304,4,256]{3,2,1,0:T(4,128)(2,1)} %wv_hbm.3, bf16[6,2048,2304]{2,1,0:T(8,128)(2,1)} %bitcast.5), custom_call_target="tpu_custom_call" | custom-call | flops 99999997952 | bytes 140000000 | tf_op jit(solution)/shard_map/stack/pallas_call | solution.py:412
  216.7 180.6 %gather.1 = (bf16[16,512,1024]{2,1,0:T(8,128)(2,1)}, bf16[16,512,1024]{2,1,0:T(8,128)(2,1)}, bf16[16,512,2304]{2,1,0:T(8,128)(2,1)}, bf16[512,2048]{1,0:T(8,128)(2,1)}, bf16[512,2304]{1,0:T(8,128)(2,1)}) custom-call(bf16[16,512,2304]{2,1,0:T(8,128)(2,1)} %stack.13.x_in, bf16[6,2304,8,256]{3,2,1,0:T(8,128)(2,1)} %wq_hbm.3, ...), custom_call_target="tpu_custom_call", output_to_operand_aliasing={{2}: (0, {})} | custom-call | flops 77309411328 | bytes 9437184 | tf_op jit(solution)/shard_map/gather/pallas_call | solution.py:636
  397.3 0.6 pad_add_fusion.blk_ref
  397.9 45.3 %causal.1 = bf16[512,2304]{1,0:T(8,128)(2,1)} custom-call(s32[2]{0:T(128)} %pad_add_fusion.blk_ref, bf16[512,2048]{1,0:T(8,128)(2,1)} %get-tuple-element.9.q_ref, bf16[8192,1024]{1,0:T(8,128)(2,1)} %bitcast.7, bf16[8192,1024]{1,0:T(8,128)(2,1)} %bitcast.8, bf16[512,2304]{1,0:T(8,128)(2,1)} %get-tuple-element.12.x_ref, bf16[6,2048,2304]{2,1,0:T(8,128)(2,1)} %bitcast.6), custom_call_target="tpu_custom_call" | custom-call | flops 30000001024 | bytes 9437184 | tf_op jit(solution)/shard_map/causal/pallas_call | solution.py:734

commit v5 on v4

--- a/solution.py
+++ b/solution.py
@@ -488,12 +488,23 @@
         return pltpu.make_async_remote_copy(src_ref=src.at[a], dst_ref=dst.at[chunk], send_sem=csend.at[i, a], recv_sem=crecv.at[i, a, hop],
                                             device_id={"cp": other}, device_id_type=MESH)
 
-    def finals():
-        copies = []
-        for i, block in enumerate((me, 2 * num_dev - 1 - me)):
-            src = wrap(lax.div(block, 2) - shift)
-            copies.append(pltpu.make_async_copy(piece(src, lax.rem(block, 2)), f_s.at[pl.ds(i * half, half)], fsem.at[i]))
-        return copies
+    def kept(i):
+        block = jnp.where(i == 0, me, 2 * num_dev - 1 - me)
+        return wrap(lax.div(block, 2) - shift), block
+
+    def early(i):
+        return lax.div(kept(i)[0], 2) != lax.rem(lax.div(me, 2) + hops, num_dev // 2)
+
+    def final(i):
+        src, block = kept(i)
+        return pltpu.make_async_copy(piece(src, lax.rem(block, 2)), f_s.at[pl.ds(i * half, half)], fsem.at[i])
+
+    def queries(i):
+        part = pl.ds(pl.multiple_of(i * half, half), half)
+        final(i).wait()
+        norm_rows(f_s.at[part], n_s.at[pl.ds(0, half)])
+        with jax.named_scope("query"):
+            q_s[part, :] = jnp.dot(n_s[:half], wq_s[...], preferred_element_type=jnp.float32).astype(jnp.bfloat16)
 
     wcopies = [pltpu.make_async_copy(w.at[layer], st, wsem.at[i]) for i, (w, st) in enumerate(((wk_hbm, wk_st), (wv_hbm, wv_st), (wq_hbm, wq_st)))]
     for cp in wcopies:
@@ -521,6 +532,20 @@
 
     @pl.loop(0, hops + 1)
     def _(hop):
+        @pl.when(hop == hops)
+        def _():
+            for way, far, h in crossings:
+                if far < hops:
+                    across(way, far, h, other).wait_recv()
+            for i in range(2):
+                pl.when(early(i))(final(i).start)
+
+            @pl.loop(0, 2)
+            def _(i):
+                @pl.when(early(i))
+                def _():
+                    queries(i)
+
         for h in range(2):
             for way in range(2):
                 last_ok = way == h
@@ -580,10 +605,10 @@
             @pl.when(hop == hops)
             @scoped("cross")
             def _():
-                for way, far, h in crossings:
-                    across(way, far, h, other).wait_recv()
-                for cp in finals():
-                    cp.start()
+                for way in range(2):
+                    across(way, hops, way, other).wait_recv()
+                for i in range(2):
+                    pl.when(jnp.logical_not(early(i)))(final(i).start)
 
             with jax.named_scope("keys"):
                 v_s[a] = jnp.dot(n_s[...], wv_s[...], preferred_element_type=jnp.float32).astype(jnp.bfloat16)
@@ -601,13 +626,14 @@
                 def _():
                     share(i, a, hop, wrap(source(a) + shift)).wait_send()
 
-    for cp in finals():
-        cp.wait()
+    @pl.loop(0, 2)
+    def _(i):
+        @pl.when(jnp.logical_not(early(i)))
+        def _():
+            queries(i)
+
     keep = pltpu.make_async_copy(f_s, x_fin, lsem.at[0])
     keep.start()
-    norm_rows(f_s, n_s)
-    with jax.named_scope("query"):
-        q_s[...] = jnp.dot(n_s[...], wq_s[...], preferred_element_type=jnp.float32).astype(jnp.bfloat16)
     last = pltpu.make_async_copy(q_s, q_hbm, lsem.at[1])
     last.start()
     last.wait()
@@ -648,15 +674,17 @@
     )(x_all, w_query, w_key, w_value)
 
 
-def causal_kernel(layer, seq, blk_ref, q_ref, k_ref, v_ref, x_ref, w_hbm, out_ref, o_s, w_s, upd_s, acc_s, top_s, tot_s, sem):
+def causal_kernel(layer, num_dev, seq, q_ref, k_ref, v_ref, x_hbm, w_hbm, out_ref, o_s, w_s, x_s, upd_s, acc_s, top_s, tot_s, sem):
     g = pl.program_id(0)
-    wcopy = pltpu.make_async_copy(w_hbm.at[layer], w_s, sem)
+    copies = [pltpu.make_async_copy(x_hbm, x_s, sem.at[0]), pltpu.make_async_copy(w_hbm.at[layer], w_s, sem.at[1])]
 
     @pl.when(g == 0)
     def _():
-        wcopy.start()
-
-    lead, trail = blk_ref[0], blk_ref[1]
+        for cp in copies:
+            cp.start()
+
+    lead = lax.axis_index("cp")
+    trail = 2 * num_dev - 1 - lead
     tile = 4 * BLK
     lanes = tot_s.shape[-1]
     per = tile // BLK
@@ -721,53 +749,51 @@
 
     @pl.when(g == pl.num_programs(0) - 1)
     def _():
-        wcopy.wait()
-        output_rows(o_s, w_s, x_ref, out_ref, upd_s)
-
-
-def causal_layer(blocks, q, k_all, v_all, x, w_out, layer):
+        for cp in copies:
+            cp.wait()
+        output_rows(o_s, w_s, x_s, out_ref, upd_s)
+
+
+def causal_layer(q, k_all, v_all, x, w_out, layer, num_dev):
     rows, dim = x.shape
     seq = k_all.shape[0]
     slots = 2 * (seq // 2 // (4 * BLK)) + 1
-    kv = pl.BlockSpec((seq, BLK), lambda g, b: (0, g))
-    row = pl.BlockSpec((rows, dim), lambda g, b: (0, 0))
+    kv = pl.BlockSpec((seq, BLK), lambda g: (0, g))
+    any_ = pl.BlockSpec(memory_space=pl.ANY)
     return pl.pallas_call(
-        functools.partial(causal_kernel, layer, seq),
-        grid_spec=pltpu.PrefetchScalarGridSpec(
-            num_scalar_prefetch=1,
-            grid=(k_all.shape[1] // BLK,),
-            in_specs=[pl.BlockSpec((rows, 2 * BLK), lambda g, b: (0, g)), kv, kv, row, pl.BlockSpec(memory_space=pl.ANY)],
-            out_specs=row,
-            scratch_shapes=[
-                pltpu.VMEM(q.shape, jnp.bfloat16),
-                pltpu.VMEM(w_out.shape[1:], jnp.bfloat16),
-                pltpu.VMEM((rows, dim), jnp.float32),
-                pltpu.VMEM((slots, 2, BLK, BLK), jnp.float32),
-                pltpu.VMEM((slots, 2, BLK, 1), jnp.float32),
-                pltpu.VMEM((slots, 2, BLK, 128), jnp.float32),
-                pltpu.SemaphoreType.DMA,
-            ],
-        ),
+        functools.partial(causal_kernel, layer, num_dev, seq),
+        grid=(k_all.shape[1] // BLK,),
+        in_specs=[pl.BlockSpec((rows, 2 * BLK), lambda g: (0, g)), kv, kv, any_, any_],
+        out_specs=pl.BlockSpec((rows, dim), lambda g: (0, 0)),
+        scratch_shapes=[
+            pltpu.VMEM(q.shape, jnp.bfloat16),
+            pltpu.VMEM(w_out.shape[1:], jnp.bfloat16),
+            pltpu.VMEM((rows, dim), jnp.bfloat16),
+            pltpu.VMEM((rows, dim), jnp.float32),
+            pltpu.VMEM((slots, 2, BLK, BLK), jnp.float32),
+            pltpu.VMEM((slots, 2, BLK, 1), jnp.float32),
+            pltpu.VMEM((slots, 2, BLK, 128), jnp.float32),
+            pltpu.SemaphoreType.DMA((2,)),
+        ],
         out_shape=jax.ShapeDtypeStruct((rows, dim), jnp.bfloat16),
         compiler_params=params(),
         cost_estimate=pl.CostEstimate(flops=30 * 10 ** 9, bytes_accessed=2 * w_out[0].size, transcendentals=0),
         name="causal",
-    )(blocks, q, k_all, v_all, x, w_out)
+    )(q, k_all, v_all, x, w_out)
 
 
 def solution(mesh):
     num_dev = mesh.shape["cp"]
 
     def per_device(hidden, w_query, w_key, w_value, w_out):
-        rank = lax.axis_index("cp")
         num_layers = w_query.shape[0]
-        rows, dim = hidden.shape
+        dim = hidden.shape[1]
         w_out = w_out.reshape(num_layers, -1, dim)
         last = num_layers - 1
         x = window_stack(hidden, w_query, w_key, w_value, w_out, last, num_dev)
         k_all, v_all, _, q, x_fin = gather_keys(x, w_query, w_key, w_value, last, last, num_dev)
-        blocks = jnp.stack([rank, 2 * num_dev - 1 - rank]).astype(jnp.int32)
-        return causal_layer(blocks, q, k_all.reshape(-1, k_all.shape[-1]), v_all.reshape(-1, v_all.shape[-1]), x_fin, w_out, last)
+        k_all, v_all = (t.reshape(-1, t.shape[-1]) for t in (k_all, v_all))
+        return causal_layer(q, k_all, v_all, x_fin, w_out, last, num_dev)
 
     row_spec = P(("dp", "cp"), None)
     return jax.shard_map(per_device, mesh=mesh, in_specs=(row_spec, P(), P(), P(), P()), out_specs=row_spec, check_vma=False)

time: 444 us -> 435 us (0.980)
  Pallas kernels: 443 us -> 434 us
    pallas_call x1, Pallas kernels: 181 us -> 176 us  [gather_keys(): pl.pallas_call(functools.partial(gather_kernel, num_dev, layer, shift), i...]
where the time goes in v5:
time: 435 us; the launch traced here: 434 us
  Pallas kernels  434 us (100%)
    pallas_call x1, Pallas kernels, window_stack(): pl.pallas_call(functools.partial(stack_kernel, num_dev, num_layers), in_s...  217 us
    pallas_call x1, Pallas kernels, gather_keys(): pl.pallas_call(functools.partial(gather_kernel, num_dev, layer, shift), i...  176 us
    pallas_call x1, Pallas kernels, causal_layer(): pl.pallas_call(functools.partial(causal_kernel, layer, num_dev, seq), gri...  41.5 us

profile of v5, /device:TPU:21, one launch (start us, length us, event | category | flops | bytes accessed | tf_op | source)
XLA Modules:
  0.0 434.4 jit_solution(5795544744428726645)
XLA Ops:
  0.0 216.7 %stack.1.x_in = bf16[16,512,2304]{2,1,0:T(8,128)(2,1)} custom-call(bf16[512,2304]{1,0:T(8,128)(2,1)} %x_hbm.1, bf16[6,2304,8,256]{3,2,1,0:T(8,128)(2,1)} %wq_hbm.3, bf16[6,2304,4,256]{3,2,1,0:T(4,128)(2,1)} %wk_hbm.3, bf16[6,2304,4,256]{3,2,1,0:T(4,128)(2,1)} %wv_hbm.3, bf16[6,2048,2304]{2,1,0:T(8,128)(2,1)} %bitcast.3), custom_call_target="tpu_custom_call" | custom-call | flops 99999997952 | bytes 140000000 | tf_op jit(solution)/shard_map/stack/pallas_call | solution.py:412
  216.7 176.0 %gather.1 = (bf16[16,512,1024]{2,1,0:T(8,128)(2,1)}, bf16[16,512,1024]{2,1,0:T(8,128)(2,1)}, bf16[16,512,2304]{2,1,0:T(8,128)(2,1)}, bf16[512,2048]{1,0:T(8,128)(2,1)}, bf16[512,2304]{1,0:T(8,128)(2,1)}) custom-call(bf16[16,512,2304]{2,1,0:T(8,128)(2,1)} %stack.1.x_in, bf16[6,2304,8,256]{3,2,1,0:T(8,128)(2,1)} %wq_hbm.3, ...), custom_call_target="tpu_custom_call", output_to_operand_aliasing={{2}: (0, {})} | custom-call | flops 77309411328 | bytes 9437184 | tf_op jit(solution)/shard_map/gather/pallas_call | solution.py:662
  392.8 41.5 %causal.1 = bf16[512,2304]{1,0:T(8,128)(2,1)} custom-call(bf16[512,2048]{1,0:T(8,128)(2,1)} %get-tuple-element.9.q_ref, bf16[8192,1024]{1,0:T(8,128)(2,1)} %bitcast.5, bf16[8192,1024]{1,0:T(8,128)(2,1)} %bitcast.6, bf16[512,2304]{1,0:T(8,128)(2,1)} %get-tuple-element.12.x_hbm, bf16[6,2048,2304]{2,1,0:T(8,128)(2,1)} %bitcast.4), custom_call_target="tpu_custom_call" | custom-call | flops 30000001024 | bytes 9437184 | tf_op jit(solution)/shard_map/causal/pallas_call | solution.py:763

commit v6 on v5

--- a/solution.py
+++ b/solution.py
@@ -302,6 +302,14 @@
                         cols = pl.ds(pl.multiple_of(j * tile, tile), tile)
                         kv[block(4 + t), cols] = dot(wkv_s[:, cols])
 
+            @pl.when((s == 0) & more & is_even)
+            def _():
+                @pl.loop(0, kv_parts)
+                def _(i):
+                    kv_wait(layer + 1, i)
+                    kv_flat(layer + 1, i)
+                    kv_next(layer + 1, i)
+
             @pl.when(s == 0)
             @scoped("h_wait")
             def _():
@@ -339,7 +347,7 @@
                 cols = pl.ds(pl.multiple_of(j * out_tile, out_tile), out_tile)
                 upd_s[:, cols] = jnp.dot(q_s[s], wo_s[:, cols], preferred_element_type=jnp.float32)
 
-            relay = (s == 1) & more
+            relay = (s == 1) & more & is_odd
 
             @pl.when(relay)
             def _():

time: 435 us -> 435 us (level)
  no operation moved by 1% of the time
where the time goes in v6:
time: 435 us; the launch traced here: 434 us
  Pallas kernels  434 us (100%)
    pallas_call x1, Pallas kernels, window_stack(): pl.pallas_call(functools.partial(stack_kernel, num_dev, num_layers), in_s...  217 us
    pallas_call x1, Pallas kernels, gather_keys(): pl.pallas_call(functools.partial(gather_kernel, num_dev, layer, shift), i...  176 us
    pallas_call x1, Pallas kernels, causal_layer(): pl.pallas_call(functools.partial(causal_kernel, layer, num_dev, seq), gri...  41.5 us

profile of v6, /device:TPU:21, one launch (start us, length us, event | category | flops | bytes accessed | tf_op | source)
XLA Modules:
  0.0 434.5 jit_solution(1034290380472759291)
XLA Ops:
  0.0 216.7 %stack.1.x_in = bf16[16,512,2304]{2,1,0:T(8,128)(2,1)} custom-call(bf16[512,2304]{1,0:T(8,128)(2,1)} %x_hbm.1, bf16[6,2304,8,256]{3,2,1,0:T(8,128)(2,1)} %wq_hbm.3, bf16[6,2304,4,256]{3,2,1,0:T(4,128)(2,1)} %wk_hbm.3, bf16[6,2304,4,256]{3,2,1,0:T(4,128)(2,1)} %wv_hbm.3, bf16[6,2048,2304]{2,1,0:T(8,128)(2,1)} %bitcast.3), custom_call_target="tpu_custom_call" | custom-call | flops 99999997952 | bytes 140000000 | tf_op jit(solution)/shard_map/stack/pallas_call | solution.py:420
  216.8 176.0 %gather.1 = (bf16[16,512,1024]{2,1,0:T(8,128)(2,1)}, bf16[16,512,1024]{2,1,0:T(8,128)(2,1)}, bf16[16,512,2304]{2,1,0:T(8,128)(2,1)}, bf16[512,2048]{1,0:T(8,128)(2,1)}, bf16[512,2304]{1,0:T(8,128)(2,1)}) custom-call(bf16[16,512,2304]{2,1,0:T(8,128)(2,1)} %stack.1.x_in, bf16[6,2304,8,256]{3,2,1,0:T(8,128)(2,1)} %wq_hbm.3, ...), custom_call_target="tpu_custom_call", output_to_operand_aliasing={{2}: (0, {})} | custom-call | flops 77309411328 | bytes 9437184 | tf_op jit(solution)/shard_map/gather/pallas_call | solution.py:670
  392.8 41.5 %causal.1 = bf16[512,2304]{1,0:T(8,128)(2,1)} custom-call(bf16[512,2048]{1,0:T(8,128)(2,1)} %get-tuple-element.9.q_ref, bf16[8192,1024]{1,0:T(8,128)(2,1)} %bitcast.5, bf16[8192,1024]{1,0:T(8,128)(2,1)} %bitcast.6, bf16[512,2304]{1,0:T(8,128)(2,1)} %get-tuple-element.12.x_hbm, bf16[6,2048,2304]{2,1,0:T(8,128)(2,1)} %bitcast.4), custom_call_target="tpu_custom_call" | custom-call | flops 30000001024 | bytes 9437184 | tf_op jit(solution)/shard_map/causal/pallas_call | solution.py:771
